TPU v7x, 128 devices: a whole 4x4x4 slice. The times are simulated.
128 devices in a mesh: seq: 8 (over y_lo, x), exp: 16 (over y_hi, z, core).
Axes of the slice: x: 4, y: 4 (y_hi: 2, y_lo: 2; y = y_hi * 2 + y_lo), z: 4, core: 2. Of those that a mesh axis runs over, the one named last changes fastest.
Arguments:
- gates: float32 [16384, 2], P(('seq', 'exp')), may hold values from 0.1 to 0.9
- expert_ids: int32 [16384, 2], P(('seq', 'exp')), may hold values from 0 to 15, all different within a row; in each aligned block of 128 rows (0 to 127, 128 to 255, ...) at most 16 rows name the same one
- saved_pre: bfloat16 [16, 2048, 2, 7168], P('exp', None, None, 'seq'), may hold values from -6 to 6
- w_down: bfloat16 [16, 7168, 4096], P('exp', 'seq'), may hold values from -0.0625 to 0.0625
- residual_grad: bfloat16 [16384, 4096], P(('seq', 'exp')), may hold values from -6 to 6
- in_weight: bfloat16 [4096, 4096], P('seq', 'exp'), may hold values from -0.09375 to 0.09375
- ssm_in: bfloat16 [16384, 4096], P('seq', 'exp'), may hold values from -0.59765625 to 0.59765625
- b_proj: bfloat16 [16384, 128], P('seq'), may hold values from -0.546875 to 0.546875
- c_proj: bfloat16 [16384, 128], P('seq'), may hold values from -0.546875 to 0.546875
- step_sizes: float32 [64, 16384], P('exp', 'seq'), may hold values from 0.05 to 4590.52
- a_log: float32 [64], P('exp'), may hold values from -12 to 0
- skip_gain: float32 [64], P('exp'), may hold values from 0.5 to 1.5
- ssm_grad: bfloat16 [16384, 4096], P('seq', 'exp'), may hold values from -6 to 6
Outputs:
- pre_grads: bfloat16 [16, 2048, 2, 7168], P('exp', None, None, 'seq')
- route_grads: float32 [16384, 2], P(('seq', 'exp'))
- b_grads: float32 [16384, 128], P(('seq', 'exp'))
- c_grads: float32 [16384, 128], P(('seq', 'exp'))
- step_grads: float32 [64, 16384], P('exp', 'seq')
Inputs may be any that keep to these rules, and one draw needn't show every extreme that they name: `expert_ids`: in each aligned block of 128 rows every expert is named by exactly 16 entries, and a row names 2 different experts.
All inputs are finite; a program needn't handle non-finite values.
Results may differ from a plain program's by a relative error of at most 0.019.
Values may be sent and summed in bfloat16 or wider, within the bound.
A program may use at most 192 MiB of HBM per device.

v0:
```python
import jax
import jax.numpy as jnp
from jax import lax
from jax.sharding import Mesh
from jax.sharding import PartitionSpec as P

TOPK = 2
HDIM = 64
SPAN = 256
EXP = ("exp_0", "exp_1", "exp_2")
SEQ_EXP = ("seq", "exp_0", "exp_1", "exp_2")


def in_blocks(array, dim, count):
    shape = array.shape
    tiles = array.reshape(*shape[:dim], count, shape[dim] // count, *shape[dim + 1 :])
    return jnp.moveaxis(tiles, dim, 0)


def summed_on_arrival(array, axis, dim):
    count = lax.axis_size(axis)
    tiles = lax.all_to_all(in_blocks(array, dim, count), axis, 0, 0, tiled=True)
    return jnp.sum(tiles, axis=0)


def copy_for_each(array, axis):
    copies = jnp.broadcast_to(array, (lax.axis_size(axis), *array.shape))
    return lax.all_to_all(copies, axis, split_axis=0, concat_axis=0, tiled=True)


def folded_in_pairs(pieces, combine):
    while len(jax.tree.leaves(pieces)[0]) > 1:
        pieces = jax.vmap(combine)(
            *(jax.tree.map(lambda part: part[side::2], pieces) for side in (0, 1))
        )
    return jax.tree.map(lambda part: part[0], pieces)


def carried_in(array, axis, combine, identity, reverse):
    count, here = (lax.axis_size(axis), lax.axis_index(axis))
    passed = jnp.arange(count) > here if reverse else jnp.arange(count) < here

    def kept(part, zero, own):
        part = jnp.where(
            passed.reshape(-1, *(1 for _ in own.shape)), part, jnp.asarray(zero, own.dtype)
        )
        return part[::-1] if reverse else part

    pieces = jax.tree.map(lambda part: copy_for_each(part, axis), array)
    return folded_in_pairs(jax.tree.map(kept, pieces, identity, array), combine)


def in_one_piece(arrays, axis, dim, along):
    ends, at = ([], 0)
    for a in arrays[:-1]:
        at += a.shape[along]
        ends.append(at)
    both = jnp.concatenate(arrays, axis=along)
    return tuple(
        jnp.split(lax.psum_scatter(both, axis, scatter_dimension=dim, tiled=True), ends, axis=along)
    )


def laid_out(tiles, dim):
    tiles = jnp.moveaxis(tiles, 0, dim)
    shape = tiles.shape
    return tiles.reshape(*shape[:dim], shape[dim] * shape[dim + 1], *shape[dim + 2 :])


def gathered_copies(array, axis, dim):
    tiles = copy_for_each(array, axis)
    return laid_out(tiles, dim)


def summed_rows(array, chips, core, dim):
    sizes = (lax.axis_size(chips), lax.axis_size(core))
    tiles = in_blocks(array, dim, sizes[0] * sizes[1])
    inside = tiles.shape[1:]
    tiles = tiles.reshape(*sizes, *inside).swapaxes(0, 1).reshape(-1, *inside)
    tiles = lax.psum_scatter(tiles, core, scatter_dimension=0, tiled=True)
    return lax.psum_scatter(tiles, chips, scatter_dimension=0, tiled=True)[0]


def span_scan(heads_input, b_values, c_values, log_decay, skip_values, start_state):
    head_count, length, head_size = heads_input.shape
    state_size = b_values.shape[1]
    blocks = length // SPAN
    x_spans = heads_input.reshape(head_count, blocks, SPAN, head_size).transpose(1, 0, 2, 3)
    b_spans = b_values.reshape(blocks, SPAN, state_size)
    c_spans = c_values.reshape(blocks, SPAN, state_size)
    g_spans = log_decay.reshape(head_count, blocks, SPAN).transpose(1, 0, 2)
    lower_mask = jnp.tril(jnp.ones((SPAN, SPAN), jnp.bool_))

    def advance(carried_state, inputs):
        x_block, b_block, c_block, g_block = inputs
        cumulative = jnp.cumsum(g_block, axis=1)
        spread = cumulative[:, :, None] - cumulative[:, None, :]
        weights = jnp.where(lower_mask, jnp.exp(-jnp.where(lower_mask, spread, 0.0)), 0.0)
        scores = jnp.dot(c_block, b_block.T)
        within = jnp.einsum("hij,ij,hjp->hip", weights, scores, x_block)
        carried = jnp.einsum("hi,in,hpn->hip", jnp.exp(-cumulative), c_block, carried_state)
        tail_decay = jnp.exp(cumulative - cumulative[:, -1:])
        fresh_state = jnp.einsum("hj,hjp,jn->hpn", tail_decay, x_block, b_block)
        next_state = jnp.exp(-cumulative[:, -1])[:, None, None] * carried_state + fresh_state
        return (next_state, within + carried)

    final_state, outputs = lax.scan(advance, start_state, (x_spans, b_spans, c_spans, g_spans))
    output = outputs.transpose(1, 0, 2, 3).reshape(head_count, length, head_size)
    return (output + skip_values[:, None, None] * heads_input, final_state)


def swiglu_grads(upstream, gate_values, saved_rows):
    gate_pre = saved_rows[:, 0, :].astype(jnp.float32)
    up_pre = saved_rows[:, 1, :].astype(jnp.float32)
    sigmoid_gate = jax.nn.sigmoid(gate_pre)
    activated = gate_pre * sigmoid_gate
    route_part = jnp.sum(activated * up_pre * upstream, axis=1)
    hidden_grad = gate_values[:, None] * upstream
    gate_grad = hidden_grad * up_pre * sigmoid_gate * (1.0 + gate_pre * (1.0 - sigmoid_gate))
    up_grad = hidden_grad * activated
    return (jnp.stack([gate_grad, up_grad], axis=1).astype(jnp.bfloat16), route_part)


def chain_join(earlier, latter):
    return (earlier[0] * latter[0], latter[0][:, None, None] * earlier[1] + latter[1])


def moe_part(moe_grad, gates, expert_ids, saved_pre, w_down):
    tokens_here = moe_grad.shape[0]
    expert_count = lax.axis_size(EXP)
    group_count = lax.axis_size("seq")
    capacity = TOPK * tokens_here // expert_count
    flat_ids = expert_ids.reshape(-1)
    onehot = (flat_ids[:, None] == jnp.arange(expert_count, dtype=jnp.int32)[None, :]).astype(
        jnp.int32
    )
    running = jnp.cumsum(onehot, axis=0)
    position = jnp.sum(onehot * running, axis=1) - 1
    target = flat_ids * capacity + position
    selector = target[:, None] == jnp.arange(expert_count * capacity, dtype=jnp.int32)[None, :]
    repeated = jnp.repeat(moe_grad, TOPK, axis=0)
    outgoing = lax.dot_general(
        selector.astype(jnp.bfloat16),
        repeated,
        (((0,), (0,)), ((), ())),
        preferred_element_type=jnp.float32,
    )
    outgoing = outgoing.astype(jnp.bfloat16).reshape(expert_count, capacity, moe_grad.shape[1])
    outgoing_gates = lax.dot_general(
        selector.astype(jnp.float32), gates.reshape(-1), (((0,), (0,)), ((), ()))
    )
    outgoing_gates = outgoing_gates.reshape(expert_count, capacity)
    weight = w_down[0]
    saved_rows = saved_pre[0]
    arrived = (
        lax.all_to_all(outgoing, EXP, split_axis=0, concat_axis=0, tiled=True),
        lax.all_to_all(
            outgoing_gates.astype(jnp.bfloat16), EXP, split_axis=0, concat_axis=0, tiled=True
        ).astype(outgoing_gates.dtype),
    )
    gathered, arrived_gates = (
        lax.all_gather(arrived[0], "seq", axis=0, tiled=True),
        lax.all_gather(arrived[1].astype(jnp.bfloat16), "seq", axis=0, tiled=True).astype(
            jnp.float32
        ),
    )
    upstream = lax.dot_general(
        gathered,
        weight,
        (((gathered.ndim - 1,), (1,)), ((), ())),
        preferred_element_type=jnp.float32,
    )
    slot_count = upstream.shape[0] * upstream.shape[1]
    pre_grad, route_part = swiglu_grads(
        upstream.reshape(slot_count, -1), arrived_gates.reshape(-1), saved_rows
    )
    route_part = route_part.reshape(group_count * expert_count, capacity)
    partial_value = summed_on_arrival(route_part, "seq", 0)
    totals = lax.all_to_all(partial_value, EXP, split_axis=0, concat_axis=0, tiled=True)
    route_grads = totals.reshape(-1)[target].reshape(tokens_here, TOPK)
    return (pre_grad[None], route_grads)


def ssm_part(ssm_in, b_proj, c_proj, step_sizes, a_log, skip_gain, ssm_grad):
    length, columns = ssm_in.shape
    head_count = columns // HDIM
    heads_input = ssm_in.astype(jnp.float32).reshape(length, head_count, HDIM).transpose(1, 0, 2)
    grads_heads = ssm_grad.astype(jnp.float32).reshape(length, head_count, HDIM).transpose(1, 0, 2)
    b_values = b_proj.astype(jnp.float32)
    c_values = c_proj.astype(jnp.float32)
    decay_rates = jnp.exp(a_log)
    log_decay = step_sizes * decay_rates[:, None]
    cumulative = jnp.cumsum(log_decay, axis=1)
    chain_total = cumulative[:, -1]
    shard_decay = jnp.exp(-chain_total)
    end_state = jnp.einsum(
        "ht,htp,tn->hpn", jnp.exp(cumulative - chain_total[:, None]), heads_input, b_values
    )
    entry_grad = jnp.einsum("ht,htp,tn->hpn", jnp.exp(-cumulative), grads_heads, c_values)
    identity = (jnp.ones_like(shard_decay), jnp.zeros_like(end_state))
    entry_state = carried_in((shard_decay, end_state), "seq", chain_join, identity, False)[1]
    exit_grad = carried_in((shard_decay, entry_grad), "seq", chain_join, identity, True)[1]

    def local_forward(inputs, b_local, c_local, log_rates):
        return span_scan(inputs, b_local, c_local, log_rates, skip_gain, entry_state)

    unused, pullback = jax.vjp(local_forward, heads_input, b_values, c_values, log_decay)
    input_heads, b_grad, c_grad, decay_grad = pullback((grads_heads, exit_grad))
    step_grads = decay_grad * decay_rates[:, None]
    x_grad = input_heads.transpose(1, 0, 2).reshape(length, columns).astype(jnp.bfloat16)
    b_grads, c_grads = in_one_piece((b_grad, c_grad), EXP, 0, 1)
    return (x_grad, b_grads, c_grads, step_grads)


def per_device(
    gates,
    expert_ids,
    saved_pre,
    w_down,
    residual_grad,
    in_weight,
    ssm_in,
    b_proj,
    c_proj,
    step_sizes,
    a_log,
    skip_gain,
    ssm_grad,
):
    x_grad, b_grads, c_grads, step_grads = ssm_part(
        ssm_in, b_proj, c_proj, step_sizes, a_log, skip_gain, ssm_grad
    )
    whole_weight = gathered_copies(in_weight, "seq", 0)
    summed = summed_rows(
        lax.dot_general(
            x_grad, whole_weight, (((1,), (1,)), ((), ())), preferred_element_type=jnp.float32
        ).astype(jnp.bfloat16),
        ("exp_0", "exp_1"),
        "exp_2",
        0,
    ).astype(jnp.float32)
    moe_grad = (residual_grad.astype(jnp.float32) + summed).astype(jnp.bfloat16)
    pre_grads, route_grads = moe_part(moe_grad, gates, expert_ids, saved_pre, w_down)
    return (pre_grads, route_grads, b_grads, c_grads, step_grads)


def solution(mesh):
    split = Mesh(
        mesh.devices.reshape(mesh.shape["seq"], 2, 4, 2), ("seq", "exp_0", "exp_1", "exp_2")
    )
    in_specs = (
        P(SEQ_EXP, None),
        P(SEQ_EXP, None),
        P(EXP, None, None, "seq"),
        P(EXP, "seq", None),
        P(SEQ_EXP, None),
        P("seq", EXP),
        P("seq", EXP),
        P("seq", None),
        P("seq", None),
        P(EXP, "seq"),
        P(EXP),
        P(EXP),
        P("seq", EXP),
    )
    out_specs = (
        P(EXP, None, None, "seq"),
        P(SEQ_EXP, None),
        P(SEQ_EXP, None),
        P(SEQ_EXP, None),
        P(EXP, "seq"),
    )
    return jax.shard_map(
        per_device, mesh=split, in_specs=in_specs, out_specs=out_specs, check_vma=False
    )
```

profile of v0, /device:TPU:1, one launch (start us, length us, event | category | flops | bytes accessed | tf_op | source)
XLA Modules:
  0.0 862.5 jit_solution(5964369956891193884)
XLA Ops:
  11.9 5.9 all-to-all-start.1
  22.1 1.9 copy.196
  24.7 2.2 copy.233
  28.1 5.1 all-to-all-start.2
  36.0 13.2 %all-to-all-done.2 = f32[8,4,64,128]{3,2,1,0:T(8,128)} async-done(((f32[8,4,64,128]{3,2,1,0:T(8,128)}), f32[8,4,64,128]{3,2,1,0:T(8,128)}, u32[]{:S(2)}, u32[]{:S(2)}) %all-to-all-start.2) | async-done | bytes 1048608 | tf_op jit(solution)/shard_map/all_to_all | solution.py:28
  50.4 3.6 all-to-all-start.3
  58.8 11.0 %all-to-all-done.3 = f32[8,4,64,128]{3,2,1,0:T(8,128)S(1)} async-done(((f32[8,4,64,128]{3,2,1,0:T(8,128)}), f32[8,4,64,128]{3,2,1,0:T(8,128)S(1)}, u32[]{:S(2)}, u32[]{:S(2)}) %all-to-all-start.3) | async-done | bytes 1048608 | tf_op jit(solution)/shard_map/all_to_all | solution.py:28
  71.3 4.3 all-to-all-start.4
  78.3 117.4 %while.65 = (s32[]{:T(128)}, f32[4,64,128]{2,1,0:T(8,128)S(1)}, f32[8,4,256,256]{3,2,1,0:T(8,128)}, bf16[8,128,256]{1,2,0:T(8,128)(2,1)}, f32[8,256,256]{2,1,0:T...) while((s32[]{:T(128)}, f32[4,64,128]{2,1,0:T(8,128)S(1)}, ...), condition=%wide.region_8.9_spmd.clone.clone.clone, body=%wide.region_5.8_spmd.clone.clone.sunk.clone | while | flops 53022744 | bytes 6271773 | solution.py:107
  109.3 1.8 bitcast_dynamic-update-slice_fusion.16
  124.0 1.8 bitcast_dynamic-update-slice_fusion.16
  199.7 193.4 %while.66 = (s32[]{:T(128)}, f32[4,64,128]{2,1,0:T(8,128)S(1)}, f32[8,4,256,64]{2,3,1,0:T(8,128)}, f32[8,256,128]{2,1,0:T(8,128)}, f32[8,256,128]{2,1,0:T(8,128)...) while((s32[]{:T(128)}, f32[4,64,128]{2,1,0:T(8,128)S(1)}, ...), condition=%wide.region_16.17_spmd.clone.clone.clone, body=%wide.region_9.16_spmd.clone.clone.sunk.clone | while | flops 170925072 | bytes 11393397 | solution.py:107
  199.7 1.8 constant_dynamic-slice_fusion.11
  202.5 1.9 fusion.194
  213.7 5.0 reduce-window.78
  219.1 2.0 fusion.200
  223.9 1.8 constant_dynamic-slice_fusion.11
  226.7 1.9 fusion.194
  237.9 5.0 reduce-window.78
  243.3 1.9 fusion.200
  248.1 1.8 constant_dynamic-slice_fusion.11
  250.9 1.9 fusion.194
  262.1 5.0 reduce-window.78
  267.5 1.9 fusion.200
  272.3 1.8 constant_dynamic-slice_fusion.11
  275.1 1.9 fusion.194
  286.2 5.0 reduce-window.78
  291.6 1.9 fusion.200
  296.4 1.8 constant_dynamic-slice_fusion.11
  299.2 1.9 fusion.194
  310.4 5.0 reduce-window.78
  315.8 2.0 fusion.200
  320.6 1.8 constant_dynamic-slice_fusion.11
  323.4 1.9 fusion.194
  334.6 5.0 reduce-window.78
  340.0 2.0 fusion.200
  344.8 1.8 constant_dynamic-slice_fusion.11
  347.6 1.9 fusion.194
  358.8 5.0 reduce-window.78
  364.2 2.0 fusion.200
  369.0 1.8 constant_dynamic-slice_fusion.11
  371.8 1.9 fusion.194
  383.0 5.0 reduce-window.78
  388.3 2.0 fusion.200
  393.2 1.9 copy.229
  395.5 9.7 %convolution_convert_fusion = bf16[2048,4096]{1,0:T(8,128)(2,1)} fusion(bf16[2048,256]{0,1:T(8,128)(2,1)S(1)} %bitcast.518, bf16[4096,256]{1,0:T(8,128)(2,1)} %bitcast.27), kind=kOutput, calls=%fused_computation.113 | convolution fusion | flops 4303355904 | bytes 19922944 | tf_op jit(solution)/shard_map/dot_general | solution.py:235
  405.2 14.0 %copy.201 = bf16[2,8,128,4096]{3,2,1,0:T(8,128)(2,1)} copy(bf16[2,8,128,4096]{3,2,0,1:T(8,128)(2,1)} %bitcast.505) | data formatting | bytes 33554432 | tf_op jit(solution)/shard_map/transpose | solution.py:79
  419.3 30.6 %reduce-scatter.4.cloned.1.call-done = bf16[8,128,4096]{2,1,0:T(8,128)(2,1)} async-done(((bf16[16,128,4096]{2,1,0:T(8,128)(2,1)}), bf16[8,128,4096]{2,1,0:T(8,128)(2,1)}) %reduce-scatter.4.cloned.1.call-update) | async-done | bytes 8388624 | tf_op jit(solution)/shard_map/reduce_scatter | solution.py:80
  451.9 116.8 %reduce-scatter.6.cloned.1.call-done = bf16[1,128,4096]{2,1,0:T(8,128)(2,1)} async-done(((bf16[8,128,4096]{2,1,0:T(8,128)(2,1)}), bf16[1,128,4096]{2,1,0:T(8,128)(2,1)}) %reduce-scatter.6.cloned.1.call-update) | async-done | bytes 1048592 | tf_op jit(solution)/shard_map/reduce_scatter | solution.py:81
  570.2 2.1 broadcast_in_dim.239
  572.3 2.2 reshape.579
  574.5 2.4 convolution_convert_fusion.1
  577.0 32.7 %all_to_all.56 = bf16[16,16,4096]{2,1,0:T(8,128)(2,1)} all-to-all(bf16[16,16,4096]{2,1,0:T(8,128)(2,1)S(1)} %bitcast.514), channel_id=1, replica_groups=mesh['seq'=8,'exp_0'=2,'exp_1'=4,'exp_2'=2] {'exp_0','exp_1','exp_2'}, dimensions={0} | all-to-all | bytes 4194304 | tf_op jit(solution)/shard_map/all_to_all | solution.py:156
  610.9 4.5 all-to-all-start
  616.0 18.8 %copy.202 = bf16[1,2048,2,896]{1,3,2,0:T(8,128)(2,1)} copy(bf16[1,2048,2,896]{3,2,1,0:T(2,128)(2,1)} %param.19) | data formatting | bytes 14680064 | tf_op args[2]
  634.8 25.3 %all-gather = bf16[128,1,16]{2,0,1:T(8,128)(2,1)S(1)} all-gather(bf16[16,1,16]{2,0,1:T(8,128)(2,1)S(1)} %copy.186), channel_id=2, replica_groups=mesh['seq'=8,'exp_0'=2,'exp_1'=4,'exp_2'=2] {'seq'}, dimensions={0}, use_global_device_ids=true | all-gather | bytes 4608 | tf_op jit(solution)/shard_map/all_gather | solution.py:163
  662.5 115.7 %all-gather.3.cloned.1.call-done = bf16[128,16,4096]{2,1,0:T(8,128)(2,1)} async-done(((bf16[16,16,4096]{2,1,0:T(8,128)(2,1)}), bf16[128,16,4096]{2,1,0:T(8,128)(2,1)}) %all-gather.3.cloned.1.call-update) | async-done | bytes 16777232 | tf_op jit(solution)/shard_map/all_gather | solution.py:162
  778.2 28.0 %fusion.80 = (bf16[1,2048,1,896]{1,3,2,0:T(8,128)(2,1)}, bf16[1,2048,1,896]{1,3,2,0:T(8,128)(2,1)}, f32[2048]{0:T(1024)S(1)}) fusion(f32[2048]{0:T(1024)S(1)} %reshape.592, bf16[2048,2,896]{0,2,1:T(8,128)(2,1)} %bitcast.516, bf16[2048,4096]{1,0:T(8,128)(2,1)} %bitcast.542, bf16[1,896,4096]{2,1,0:T(8,128)(2,1)} %param.20), kind=kOutput, calls=%fused_computation.136 | convolution fusion | flops 15067248640 | bytes 38813696 | tf_op jit(solution)/shard_map/dot_general | solution.py:167
  807.0 3.3 all-to-all-start.6
  811.9 3.4 all-to-all-done.6
  817.2 8.7 %all-to-all-start.7 = ((f32[16,1,16]{2,1,0:T(1,128)}), f32[16,1,16]{2,1,0:T(1,128)S(1)}, u32[]{:S(2)}, u32[]{:S(2)}) async-start(f32[16,1,16]{2,1,0:T(1,128)} %bitcast.43), calls=%async_computation.9 | async-start | bytes 16384 | tf_op jit(solution)/shard_map/all_to_all | solution.py:179
  825.9 6.8 pad_maximum_fusion
  832.7 18.7 %copy.206 = bf16[1,2048,2,896]{3,2,1,0:T(2,128)(2,1)} copy(bf16[1,2048,2,896]{1,3,2,0:T(8,128)(2,1)} %pad_maximum_fusion) | data formatting | bytes 14680064
  852.6 1.9 gather_fusion
  (590 shorter events, 262.1 us)
Async XLA Ops:
  11.9 15.0 %all-to-all-start.1 = ((f32[8,1,4]{2,1,0:T(1,128)}), f32[8,1,4]{2,1,0:T(1,128)S(1)}, u32[]{:S(2)}, u32[]{:S(2)}) async-start(f32[8,1,4]{2,1,0:T(1,128)} %broadcast_in_dim.223), calls=%async_computation.1 | async-start | bytes 8192 | tf_op jit(solution)/shard_map/all_to_all | solution.py:28
  22.1 2.2 copy-start.3
  26.9 8.9 %copy-start.8 = (f32[4,2048]{1,0:T(4,128)S(1)}, f32[4,2048]{1,0:T(4,128)}, u32[]{:S(2)}) copy-start(f32[4,2048]{1,0:T(4,128)} %param.26) | copy-start | bytes 98308
  28.1 21.1 %all-to-all-start.2 = ((f32[8,4,64,128]{3,2,1,0:T(8,128)}), f32[8,4,64,128]{3,2,1,0:T(8,128)}, u32[]{:S(2)}, u32[]{:S(2)}) async-start(f32[8,4,64,128]{3,2,1,0:T(8,128)} %broadcast_in_dim.226), calls=%async_computation.2 | async-start | bytes 2097152 | tf_op jit(solution)/shard_map/all_to_all | solution.py:28
  36.0 33.7 %copy-start.7 = (bf16[512,256]{1,0:T(8,128)(2,1)S(1)}, bf16[512,256]{1,0:T(8,128)(2,1)}, u32[]{:S(2)}) copy-start(bf16[512,256]{1,0:T(8,128)(2,1)} %param.22) | copy-start | bytes 786436
  50.4 19.4 %all-to-all-start.3 = ((f32[8,4,64,128]{3,2,1,0:T(8,128)}), f32[8,4,64,128]{3,2,1,0:T(8,128)S(1)}, u32[]{:S(2)}, u32[]{:S(2)}) async-start(f32[8,4,64,128]{3,2,1,0:T(8,128)} %broadcast_in_dim.230), calls=%async_computation.3 | async-start | bytes 2097152 | tf_op jit(solution)/shard_map/all_to_all | solution.py:28
  69.7 5.9 copy-start
  71.3 324.1 %all-to-all-start.4 = ((bf16[8,512,256]{2,1,0:T(8,128)(2,1)}), bf16[8,512,256]{2,1,0:T(8,128)(2,1)}, u32[]{:S(2)}, u32[]{:S(2)}) async-start(bf16[8,512,256]{2,1,0:T(8,128)(2,1)} %broadcast_in_dim.238), calls=%async_computation.4 | async-start | bytes 4194304 | tf_op jit(solution)/shard_map/all_to_all | solution.py:28
  75.7 374.2 %reduce-scatter.4.cloned.1.call-start = ((), (), s32[]{:S(2)}) async-start(), calls=%async_computation.11 | async-start | bytes 25165824 | tf_op jit(solution)/shard_map/reduce_scatter | solution.py:80
  78.3 117.4 %copy-start.4 = (f32[4,4,64,128]{3,2,1,0:T(8,128)S(1)}, f32[4,4,64,128]{3,2,1,0:T(8,128)}, u32[]{:S(2)}) copy-start(f32[4,4,64,128]{3,2,1,0:T(8,128)} %get-tuple-element.1303) | copy-start | bytes 1572868
  78.3 117.4 %copy-start.5 = (f32[4,4,64,128]{3,2,1,0:T(8,128)S(1)}, f32[4,4,64,128]{3,2,1,0:T(8,128)}, u32[]{:S(2)}) copy-start(f32[4,4,64,128]{3,2,1,0:T(8,128)} %get-tuple-element.1304) | copy-start | bytes 1572868
  78.3 117.6 %copy-start.10 = (f32[4]{0:T(128)S(1)}, f32[4]{0:T(128)}, u32[]{:S(2)}) copy-start(f32[4]{0:T(128)} %slice_reduce_fusion.3) | copy-start | bytes 52
  393.2 1.9 copy-start.12
  419.3 149.5 %reduce-scatter.6.cloned.1.call-start = ((), (), s32[]{:S(2)}) async-start(), calls=%async_computation.12 | async-start | bytes 9437184 | tf_op jit(solution)/shard_map/reduce_scatter | solution.py:81
  449.9 0.7 copy-start.9
  449.9 118.8 %copy-start.6 = (bf16[128,4096]{1,0:T(8,128)(2,1)S(1)}, bf16[128,4096]{1,0:T(8,128)(2,1)}, u32[]{:S(2)}) copy-start(bf16[128,4096]{1,0:T(8,128)(2,1)} %param.21) | copy-start | bytes 3145732
  450.0 328.2 %all-gather.3.cloned.1.call-start = ((), (), s32[]{:S(2)}) async-start(), calls=%async_computation.13 | async-start | bytes 18874368 | tf_op jit(solution)/shard_map/all_gather | solution.py:162
  577.0 32.7 %copy-start.11 = (f32[128,2]{0,1:T(2,128)S(1)}, f32[128,2]{0,1:T(2,128)}, u32[]{:S(2)}) copy-start(f32[128,2]{0,1:T(2,128)} %param.17) | copy-start | bytes 3076
  610.9 23.9 %all-to-all-start = ((bf16[16,1,16]{2,1,0:T(2,128)(2,1)}), bf16[16,1,16]{2,1,0:T(2,128)(2,1)S(1)}, u32[]{:S(2)}, u32[]{:S(2)}) async-start(bf16[16,1,16]{2,1,0:T(2,128)(2,1)} %copy.185), calls=%async_computation | async-start | bytes 16384 | tf_op jit(solution)/shard_map/all_to_all | solution.py:157
  615.5 194.9 %reduce-scatter.8.cloned.1.call-start = ((), (), s32[]{:S(2)}) async-start(), calls=%async_computation.14 | async-start | bytes 2228224 | tf_op jit(solution)/shard_map/reduce_scatter | solution.py:60
  616.0 44.2 %copy-start.1 = (f32[8,256,128]{2,1,0:T(8,128)S(1)}, f32[8,256,128]{2,1,0:T(8,128)}, u32[]{:S(2)}) copy-start(f32[8,256,128]{2,1,0:T(8,128)} %get-tuple-element.751) | copy-start | bytes 3145732
  616.0 44.2 %copy-start.2 = (f32[8,256,128]{2,1,0:T(8,128)S(1)}, f32[8,256,128]{2,1,0:T(8,128)}, u32[]{:S(2)}) copy-start(f32[8,256,128]{2,1,0:T(8,128)} %get-tuple-element.752) | copy-start | bytes 3145732
  807.0 8.3 all-to-all-start.6
  817.2 34.2 %all-to-all-start.7 = ((f32[16,1,16]{2,1,0:T(1,128)}), f32[16,1,16]{2,1,0:T(1,128)S(1)}, u32[]{:S(2)}, u32[]{:S(2)}) async-start(f32[16,1,16]{2,1,0:T(1,128)} %bitcast.43), calls=%async_computation.9 | async-start | bytes 16384 | tf_op jit(solution)/shard_map/all_to_all | solution.py:179
Sparse Core Ops, SparseCore 0:
  419.4 30.5 reduce-scatter.3
  453.7 114.9 reduce-scatter.5
  609.8 168.3 all-gather.2
Sparse Core Ops, SparseCore 1:
  662.6 147.6 reduce-scatter.7
where the time goes:
time: 869 us; the launch traced here: 862 us
  waiting for transfers between devices  291 us (33%)
  local copies, waits for them, and re-layouts  156 us (18%)
  matrix products  153 us (18%)
  other arithmetic  152 us (17%)
  blocking collectives  58 us (7%)
  starting transfers between devices  36 us (4%)
  between operations  15.7 us (2%)
    reduce_scatter x1, waiting for transfers between devices, summed_rows(): return lax.psum_scatter(tiles, chips, scatter_dimension=0, tiled=True)[0]  117 us
    all_gather x1, waiting for transfers between devices, moe_part(): lax.all_gather(arrived[0], 'seq', axis=0, tiled=True)  116 us
    another operation x54, other arithmetic  53.7 us
    unnamed x41, local copies, waits for them, and re-layouts  47.9 us
    dynamic_update_slice x40, other arithmetic, span_scan(): lax.scan(advance, start_state, (x_spans, b_spans, c_spans, g_spans))  43.9 us
    dot_general x24, matrix products, advance(): scores = jnp.dot(c_block, b_block.T)  34.3 us
    all_to_all x1, blocking collectives, moe_part(): lax.all_to_all(outgoing, EXP, split_axis=0, concat_axis=0, tiled=True)  32.7 us
    dot_general x16, matrix products, advance(): within = jnp.einsum('hij,ij,hjp->hip', weights, scores, x_block)  31 us
  transfers between devices with their start and end apart: 11, of which 6 were waited for; matrix products, arithmetic and copies ran while one was open for 48% of the time, Pallas kernels for 0%

commit v1 on v0

v1 whole, which is shorter than its diff:
```python
import functools

import jax
import jax.numpy as jnp
from jax import lax
from jax.experimental import pallas as pl
from jax.experimental.pallas import tpu as pltpu
from jax.sharding import Mesh
from jax.sharding import PartitionSpec as P

TOPK = 2
HDIM = 64
SPAN = 256
CHIPS = ("exp_0", "exp_1")
CORE = "exp_2"
EXP = ("exp_0", "exp_1", "exp_2")
SEQ_EXP = ("seq", "exp_0", "exp_1", "exp_2")
F32 = jnp.float32
BF16 = jnp.bfloat16
MESH = pl.DeviceIdType.MESH


def nn(a, b):
    return lax.dot_general(a, b, (((1,), (0,)), ((), ())), preferred_element_type=F32)


def nt(a, b):
    return lax.dot_general(a, b, (((1,), (1,)), ((), ())), preferred_element_type=F32)


def tn(a, b):
    return lax.dot_general(a, b, (((0,), (0,)), ((), ())), preferred_element_type=F32)


def over_lanes(columns):
    rows, heads = columns.shape
    lane = lax.broadcasted_iota(jnp.int32, (rows, 2 * HDIM), 1)
    return jnp.concatenate(
        [
            jnp.where(lane < HDIM, columns[:, h : h + 1], columns[:, h + 1 : h + 2])
            for h in range(0, heads, 2)
        ],
        axis=1,
    )


def decays(lcol_ref):
    running = lcol_ref[...]
    last = running[SPAN - 1 : SPAN, :]
    return over_lanes(jnp.exp(-running)), over_lanes(jnp.exp(running - last))


def barrier_with(peers):
    semaphore = pltpu.get_barrier_semaphore()
    for peer in peers:
        pl.semaphore_signal(semaphore, inc=1, device_id=peer, device_id_type=MESH)
    pl.semaphore_wait(semaphore, len(peers))


ORDERS = ("xyz", "yzx", "zxy", "xzy", "yxz", "zyx")
UNIT = 16


class Torus:
    def __init__(self):
        seq = lax.axis_index("seq")
        self.at = {
            "x": lax.rem(seq, 4),
            "y": lax.axis_index("exp_0") * 2 + lax.div(seq, 4),
            "z": lax.axis_index("exp_1"),
        }

    def device(self, dim, step):
        at = dict(self.at)
        at[dim] = lax.rem(at[dim] + (step + 4), 4)
        return {"seq": lax.rem(at["y"], 2) * 4 + at["x"], "exp_0": lax.div(at["y"], 2), "exp_1": at["z"]}


class Gather:
    def __init__(self, torus, own_ref, out_ref, send_sem, recv_sem):
        self.torus, self.own, self.out = torus, own_ref, out_ref
        self.send_sem, self.recv_sem = send_sem, recv_sem
        units = own_ref.shape[0] // UNIT
        count = len(ORDERS)
        ends = [units * k // count * UNIT for k in range(count + 1)]
        self.rows = [(ends[k], ends[k + 1] - ends[k]) for k in range(count)]

    def block(self, stream, phase, step, start, size):
        order = ORDERS[stream]
        at = []
        for dim in "xyz":
            k = order.index(dim)
            if k < phase:
                at.append(slice(None))
            elif k == phase:
                at.append(lax.rem(self.torus.at[dim] + (step + 4), 4))
            else:
                at.append(self.torus.at[dim])
        return self.out.at[(*at, pl.ds(start, size), slice(None))]

    def copies(self, stream, step, back=False):
        phase, second = step // 2, step % 2
        dim = ORDERS[stream][phase]
        start, size = self.rows[stream]
        half = (size // UNIT + 1) // 2 * UNIT
        made = []
        for side, way in enumerate((1, -1)):
            if not second:
                span, hop = (start, size), 0
            else:
                span = (start, half) if side == 0 else (start + half, size - half)
                hop = -way
            sent = self.block(stream, phase, hop, *span)
            here = sent
            if step == 0:
                sent = self.own.at[pl.ds(*span), :]
            common = dict(
                send_sem=self.send_sem.at[stream, step, side],
                recv_sem=self.recv_sem.at[stream, step, side],
                device_id=self.torus.device(dim, way),
                device_id_type=MESH,
            )
            if back:
                sent = here = self.block(stream, phase, hop - way, *span)
            made.append(pltpu.make_async_remote_copy(src_ref=sent, dst_ref=here, **common))
        return made

    def start(self, stream, step):
        for copy in self.copies(stream, step):
            copy.start()

    def arrived(self, stream, step):
        for copy in self.copies(stream, step, back=True):
            copy.wait_recv()

    def advance(self, step, streams):
        for stream in streams:
            if step > 0:
                self.arrived(stream, step - 1)
            if step < 6:
                self.start(stream, step)

    def drain(self):
        for stream in range(len(ORDERS)):
            for step in range(6):
                for copy in self.copies(stream, step):
                    copy.wait_send()


def ssm_kernel(
    w_ref, x_ref, g_ref, b_ref, c_ref, lcol_ref, lrow_ref, whole_ref, before_ref, tail_ref, skip_ref, rate_ref,
    all_ref, dx_ref, dbc_ref, dq_ref,
    s_all, g_all, s_acc, g_acc, ends, got, dx_all,
    own_sem, w_send, w_recv, s_send, s_recv, x_send, x_recv,
):
    chunks = s_all.shape[0]
    parts = got.shape[0]
    width = x_ref.shape[1]
    heads = width // HDIM
    torus = Torus()
    me = lax.axis_index("seq")
    place = lax.axis_index("exp_0") * 4 + lax.axis_index("exp_1")

    def in_part(offset):
        return lax.rem(me + offset, parts)

    def chip_at(index):
        return {"exp_0": lax.div(index, 4), "exp_1": lax.rem(index, 4)}

    across_y = {"seq": lax.rem(me + 4, 8), "exp_0": 1 - lax.axis_index("exp_0")}
    barrier_with(
        [{"seq": in_part(o)} for o in range(1, parts)]
        + [chip_at(lax.rem(place + o, chunks)) for o in range(1, chunks)]
        + [across_y]
    )
    gather = Gather(torus, w_ref, all_ref, w_send, w_recv)
    streams = range(len(ORDERS))
    gather.advance(0, streams)
    here = torus.at
    own = pltpu.make_async_copy(w_ref, all_ref.at[here["x"], here["y"], here["z"]], own_sem.at[0])
    own.start()

    def rows_of(chunk):
        return pl.ds(pl.multiple_of(chunk * SPAN, SPAN), SPAN)

    s_acc[...] = jnp.zeros_like(s_acc)
    g_acc[...] = jnp.zeros_like(g_acc)

    def states(chunk, carry):
        rows = rows_of(chunk)
        from_start, to_end = decays(lcol_ref.at[rows])
        fresh = tn(b_ref[rows, :], (x_ref[rows, :].astype(F32) * to_end).astype(BF16))
        back = tn(c_ref[rows, :], (g_ref[rows, :].astype(F32) * from_start).astype(BF16))
        s_all[chunk] = fresh
        g_all[chunk] = back
        s_acc[...] = s_acc[...] * whole_ref[chunk] + fresh
        g_acc[...] = g_acc[...] + before_ref[chunk] * back
        return carry

    lax.fori_loop(0, chunks, states, 0)
    ends[0, :128, :] = s_acc[...].astype(BF16)
    ends[1, :128, :] = g_acc[...].astype(BF16)
    ends[0, 128:, :] = tail_ref[...]
    ends[1, 128:, :] = tail_ref[...]

    def to_part(offset, back=False):
        peer = in_part(offset)
        source = in_part(parts - offset)
        common = dict(
            send_sem=s_send.at[offset - 1], recv_sem=s_recv.at[offset - 1], device_id={"seq": peer}, device_id_type=MESH
        )
        which = jnp.where(peer > me, 0, 1)
        if back:
            return pltpu.make_async_remote_copy(src_ref=got.at[source], dst_ref=got.at[source], **common)
        return pltpu.make_async_remote_copy(src_ref=ends.at[which], dst_ref=got.at[me], **common)

    for offset in range(1, parts):
        to_part(offset).start()
    own.wait()
    gather.advance(1, streams)
    got[me] = jnp.zeros(got.shape[1:], BF16)
    for offset in range(1, parts):
        to_part(offset, back=True).wait_recv()
    gather.advance(2, streams)

    def decay_of(m):
        return got[m, 128:129, :].astype(F32) + got[m, 129:130, :].astype(F32)

    state = jnp.zeros((128, width), F32)
    for m in range(parts):
        state = jnp.where(m < me, decay_of(m) * state + got[m, :128, :].astype(F32), state)
    for k in range(chunks):
        fresh = s_all[k]
        s_all[k] = state
        state = state * whole_ref[k] + fresh
    state = jnp.zeros((128, width), F32)
    for m in reversed(range(parts)):
        state = jnp.where(m > me, decay_of(m) * state + got[m, :128, :].astype(F32), state)
    for k in reversed(range(chunks)):
        fresh = g_all[k]
        g_all[k] = state
        state = state * whole_ref[k] + fresh

    row = lax.broadcasted_iota(jnp.int32, (SPAN, SPAN), 0)
    col = lax.broadcasted_iota(jnp.int32, (SPAN, SPAN), 1)
    head_of = lax.broadcasted_iota(jnp.int32, (8, width), 1) // HDIM
    pick = (head_of == lax.broadcasted_iota(jnp.int32, (8, width), 0)).astype(F32)
    pick_half = pick.astype(BF16)

    def to_chip(turn, back=False):
        target = lax.rem(place + 1 + turn, chunks)
        source = lax.rem(place + (chunks - 1) - turn, chunks)
        common = dict(
            send_sem=x_send.at[turn], recv_sem=x_recv.at[turn], device_id=chip_at(target), device_id_type=MESH
        )
        if back:
            return pltpu.make_async_remote_copy(src_ref=dx_ref.at[source], dst_ref=dx_ref.at[source], **common)
        return pltpu.make_async_remote_copy(src_ref=dx_all.at[target], dst_ref=dx_ref.at[place], **common)

    def grads(turn, carry):
        chunk = lax.rem(place + 1 + turn, chunks)
        rows = rows_of(chunk)
        x = x_ref[rows, :]
        g = g_ref[rows, :]
        b = b_ref[rows, :]
        c = c_ref[rows, :]
        lcol = lcol_ref[rows, :]
        lrow = lrow_ref[:, rows]
        s_in = s_all[chunk]
        g_out = g_all[chunk]
        s_half = s_in.astype(BF16)
        g_half = g_out.astype(BF16)
        upper = row <= col
        strict = row < col
        from_row = (row >= col).astype(F32).astype(BF16)
        before_row = strict.astype(F32).astype(BF16)
        bc = nt(b, c)
        dx = jnp.zeros((SPAN, width), F32)
        pairs = jnp.zeros((SPAN, SPAN), F32)
        inside = []
        for h in range(heads):
            mine = pick_half[h : h + 1, :]
            m = nt(x * mine, g)
            w = jnp.exp(jnp.where(upper, lcol[:, h : h + 1] - lrow[h : h + 1, :], -1e30))
            a1 = w * bc
            pairs = pairs + w * m
            dx = dx + nn(a1.astype(BF16), g * mine)
            p = jnp.where(strict, a1 * m, 0.0).astype(BF16)
            inside.append(jnp.sum(jnp.where(strict, nn(p, from_row), 0.0), axis=0, keepdims=True))
        from_start, to_end = decays(lcol_ref.at[rows])
        ge = (g.astype(F32) * from_start).astype(BF16)
        xe = (x.astype(F32) * to_end).astype(BF16)
        pairs_half = pairs.astype(BF16)
        z = nn(c, s_half)
        v = nn(b, g_half)
        dbc_ref[rows, :128] = nn(pairs_half, c) + nt(xe, g_half)
        dbc_ref[rows, 128:] = tn(pairs_half, b) + nt(ge, s_half)
        dx_all[chunk] = (dx + to_end * v + skip_ref[...] * g.astype(F32)).astype(BF16)

        @pl.when(turn < chunks - 1)
        def _():
            to_chip(turn).start()

        rc = nt(pick_half, (ge.astype(F32) * z).astype(BF16))
        cc = nt(pick_half, (xe.astype(F32) * v).astype(BF16))
        across = jnp.sum(s_in * g_out, axis=0, keepdims=True) * whole_ref[chunk]
        ones = jnp.ones((width, SPAN), BF16)
        dq = nn(rc.astype(BF16), from_row) + nn(cc.astype(BF16), before_row) + nn((pick * across).astype(BF16), ones)
        for h in range(heads):
            dq_ref[h : h + 1, rows] = -(dq[h : h + 1, :] + inside[h]) * rate_ref[h : h + 1, :]
        for step, after in STEPS_AFTER:

            @pl.when(turn == after)
            def _(step=step):
                gather.advance(step, streams)

        return carry

    lax.fori_loop(0, chunks, grads, 0)
    mine = pltpu.make_async_copy(dx_all.at[place], dx_ref.at[place], own_sem.at[0])
    mine.start()
    for step in LAST_STEPS:
        gather.advance(step, streams)
    mine.wait()
    for turn in range(chunks - 1):
        to_chip(turn, back=True).wait_recv()
        to_chip(turn).wait_send()
    for offset in range(1, parts):
        to_part(offset).wait_send()
    gather.drain()


STEPS_AFTER = ((3, 1), (4, 3))
LAST_STEPS = (5, 6)


def ssm_part(in_weight, ssm_in, b_proj, c_proj, step_sizes, a_log, skip_gain, ssm_grad):
    length, width = ssm_in.shape
    heads = width // HDIM
    chunks = length // SPAN
    parts = lax.axis_size("seq")
    rates = jnp.exp(a_log)
    steps = (step_sizes * rates[:, None]).reshape(heads * chunks, SPAN)
    at = jnp.arange(SPAN)
    lrow = jnp.dot(steps, (at[:, None] <= at[None, :]).astype(F32), precision=lax.Precision.HIGHEST)
    totals = lrow[:, -1].reshape(heads, chunks)
    lrow = lrow.reshape(heads, length)
    lcol = lrow.T
    whole = jnp.repeat(jnp.exp(-totals).T, HDIM, axis=1).reshape(chunks, 1, width)
    sums = jnp.cumsum(totals, axis=1)
    before = jnp.repeat(jnp.exp(-(sums - totals)).T, HDIM, axis=1).reshape(chunks, 1, width)
    device_decay = jnp.repeat(jnp.exp(-sums[:, -1]), HDIM)
    skip = jnp.repeat(skip_gain, HDIM).reshape(1, width)
    high = device_decay.astype(BF16)
    low = (device_decay - high.astype(F32)).astype(BF16)
    tail = jnp.pad(jnp.stack([high, low]), ((0, 14), (0, 0)))
    vmem = pl.BlockSpec(memory_space=pltpu.VMEM)
    hbm = pl.BlockSpec(memory_space=pl.ANY)
    streams = len(ORDERS)
    dma = pltpu.SemaphoreType.DMA
    return pl.pallas_call(
        ssm_kernel,
        out_shape=(
            jax.ShapeDtypeStruct((4, 4, 4, *in_weight.shape), BF16),
            jax.ShapeDtypeStruct((chunks, SPAN, width), BF16),
            jax.ShapeDtypeStruct((length, 256), F32),
            jax.ShapeDtypeStruct((heads, length), F32),
        ),
        in_specs=[vmem] * 12,
        out_specs=(hbm, hbm, vmem, vmem),
        scratch_shapes=[
            pltpu.VMEM((chunks, 128, width), F32),
            pltpu.VMEM((chunks, 128, width), F32),
            pltpu.VMEM((128, width), F32),
            pltpu.VMEM((128, width), F32),
            pltpu.VMEM((2, 144, width), BF16),
            pltpu.VMEM((parts, 144, width), BF16),
            pltpu.VMEM((chunks, SPAN, width), BF16),
            dma((1,)),
            dma((streams, 6, 2)),
            dma((streams, 6, 2)),
            dma((parts - 1,)),
            dma((parts - 1,)),
            dma((chunks - 1,)),
            dma((chunks - 1,)),
        ],
        compiler_params=pltpu.CompilerParams(
            collective_id=1, has_side_effects=True, vmem_limit_bytes=48 * 2**20
        ),
        name="ssm",
    )(in_weight, ssm_in, ssm_grad, b_proj, c_proj, lcol, lrow, whole, before, tail, skip, rates[:, None])


def project_kernel(core_ref, x_ref, w_ref, keep_ref, send_ref, total):
    core = core_ref[0]
    half = keep_ref.shape[0]
    width = x_ref.shape[2]
    acc = jnp.zeros(total.shape, F32)
    for k in range(x_ref.shape[0]):
        acc = acc + nt(x_ref[k], w_ref[0, k // 4, 0, k % 4])
    total[...] = acc
    keep_ref[...] = total[pl.ds(pl.multiple_of(core * half, half), half), :].astype(BF16)
    send_ref[...] = total[pl.ds(pl.multiple_of((1 - core) * half, half), half), :].astype(BF16)


def project(x_all, w_all):
    blocks, tokens, width = x_all.shape
    rows = w_all.shape[3]
    w_all = w_all.reshape(4, 2, 2, 4, rows, width)
    half = jax.ShapeDtypeStruct((tokens // 2, 8 * rows), BF16)
    return pl.pallas_call(
        project_kernel,
        grid=(8,),
        out_shape=(half, half),
        in_specs=[
            pl.BlockSpec(memory_space=pltpu.SMEM),
            pl.BlockSpec((blocks, tokens, width), lambda i: (0, 0, 0)),
            pl.BlockSpec((1, 2, 1, 4, rows, width), lambda i: (i % 4, 0, i // 4, 0, 0, 0)),
        ],
        out_specs=(pl.BlockSpec((tokens // 2, rows), lambda i: (0, i)),) * 2,
        scratch_shapes=[pltpu.VMEM((tokens, rows), F32)],
        compiler_params=pltpu.CompilerParams(dimension_semantics=("arbitrary",)),
        name="project",
    )(lax.axis_index(CORE).reshape(1).astype(jnp.int32), x_all, w_all)


def expert_kernel(a_ref, w_ref, saved_ref, pre_ref, route_ref):
    rows = a_ref.shape[0] * a_ref.shape[1]
    upstream = nt(a_ref[...].reshape(rows, a_ref.shape[2]), w_ref[0])
    gate_pre = saved_ref[:, 0, :].astype(F32)
    up_pre = saved_ref[:, 1, :].astype(F32)
    sig = jax.nn.sigmoid(gate_pre)
    act = gate_pre * sig
    up_grad = upstream * act
    gate_grad = upstream * up_pre * sig * (1.0 + gate_pre * (1.0 - sig))
    pre_ref[:, 0, :] = gate_grad.astype(BF16)
    pre_ref[:, 1, :] = up_grad.astype(BF16)
    route_ref[...] = nt(jnp.ones((8, up_pre.shape[1]), BF16), (up_grad * up_pre).astype(BF16))


def expert_part(gathered, w_down, saved_pre):
    parts, own, d = gathered.shape
    slots, _, hidden = saved_pre.shape[1:]
    step = 256
    per = step // own
    return pl.pallas_call(
        expert_kernel,
        grid=(slots // step,),
        out_shape=(
            jax.ShapeDtypeStruct((slots, 2, hidden), BF16),
            jax.ShapeDtypeStruct((8, slots), F32),
        ),
        in_specs=[
            pl.BlockSpec((per, own, d), lambda i: (i, 0, 0)),
            pl.BlockSpec((1, hidden, d), lambda i: (0, 0, 0)),
            pl.BlockSpec((step, 2, hidden), lambda i: (i, 0, 0)),
        ],
        out_specs=(
            pl.BlockSpec((step, 2, hidden), lambda i: (i, 0, 0)),
            pl.BlockSpec((8, step), lambda i: (0, i)),
        ),
        compiler_params=pltpu.CompilerParams(
            dimension_semantics=("arbitrary",), vmem_limit_bytes=60 * 2**20
        ),
        name="experts",
    )(gathered, w_down, saved_pre[0])


def per_device(
    gates, expert_ids, saved_pre, w_down, residual_grad, in_weight, ssm_in, b_proj, c_proj, step_sizes, a_log, skip_gain, ssm_grad
):
    w_all, x_all, bc_grads, step_grads = ssm_part(
        in_weight, ssm_in, b_proj, c_proj, step_sizes, a_log, skip_gain, ssm_grad
    )
    tokens_here, d = residual_grad.shape
    experts = lax.axis_size(EXP)
    parts = lax.axis_size("seq")
    capacity = TOPK * tokens_here // experts
    bc_grads = lax.psum_scatter(bc_grads, EXP, scatter_dimension=0, tiled=True)
    b_grads, c_grads = bc_grads[:, :128], bc_grads[:, 128:]
    keep, send = project(x_all, w_all)
    other = lax.ppermute(send, CORE, [(0, 1), (1, 0)])
    moe_grad = (residual_grad.astype(F32) + keep.astype(F32) + other.astype(F32)).astype(BF16)
    flat_ids = expert_ids.reshape(-1)
    onehot = (flat_ids[:, None] == jnp.arange(experts, dtype=jnp.int32)[None, :]).astype(jnp.int32)
    position = jnp.sum(onehot * jnp.cumsum(onehot, axis=0), axis=1) - 1
    target = flat_ids * capacity + position
    selector = target[:, None] == jnp.arange(experts * capacity, dtype=jnp.int32)[None, :]
    by_token = selector.reshape(tokens_here, TOPK, -1)
    slot_gates = jnp.sum(by_token * gates[:, :, None], axis=(0, 1))
    rows = tn(jnp.any(by_token, axis=1).astype(BF16), moe_grad)
    outgoing = (rows * slot_gates[:, None]).astype(BF16).reshape(experts, capacity, d)
    arrived = lax.all_to_all(outgoing, EXP, 0, 0, tiled=True).reshape(experts * capacity, d)
    gathered = lax.all_gather(arrived, "seq", axis=0, tiled=False)
    pre_grads, route = expert_part(gathered, w_down, saved_pre)
    route = route[0].reshape(parts * experts, capacity)
    route = lax.all_to_all(route, SEQ_EXP, 0, 0, tiled=True)
    totals = jnp.sum(route.reshape(parts, experts * capacity), axis=0)
    route_grads = totals[target].reshape(tokens_here, TOPK) / gates
    return (pre_grads[None], route_grads, b_grads, c_grads, step_grads)


def solution(mesh):
    split = Mesh(mesh.devices.reshape(mesh.shape["seq"], 2, 4, 2), ("seq", "exp_0", "exp_1", "exp_2"))
    in_specs = (
        P(SEQ_EXP, None), P(SEQ_EXP, None), P(EXP, None, None, "seq"), P(EXP, "seq", None), P(SEQ_EXP, None), P("seq", EXP),
        P("seq", EXP), P("seq", None), P("seq", None), P(EXP, "seq"), P(EXP), P(EXP), P("seq", EXP),
    )
    out_specs = (P(EXP, None, None, "seq"), P(SEQ_EXP, None), P(SEQ_EXP, None), P(SEQ_EXP, None), P(EXP, "seq"))
    return jax.shard_map(per_device, mesh=split, in_specs=in_specs, out_specs=out_specs, check_vma=False)
```

time: 869 us -> 406 us (0.47)
  matrix products: 153 us -> 2.19 us
  other arithmetic: 152 us -> 3.1 us
  Pallas kernels: 0 us -> 144 us
  local copies, waits for them, and re-layouts: 156 us -> 16.2 us
  waiting for transfers between devices: 291 us -> 179 us
  blocking collectives: 58 us -> 31.6 us
  starting transfers between devices: 36 us -> 13.4 us
    dot_general x94 -> x2, matrix products: 153 us -> 2.19 us  [the longest x1 1.99 us: tn(): lax.dot_general(a, b, (((0,), (0,)), ((), ())), preferred_element_type=F32)]
    reduce_scatter x3 -> x1, waiting for transfers between devices: 147 us -> 0.03 us  [per_device(): bc_grads = lax.psum_scatter(bc_grads, EXP, scatter_dimension=0, tiled=True)]
    pallas_call x0 -> x3, Pallas kernels: none -> 144 us  [the longest x1 93 us: ssm_part(): pl.pallas_call(ssm_kernel, out_shape=(jax.ShapeDtypeStruct((4, 4, 4, *in_...]
    another operation x55 -> x4, other arithmetic: 60.5 us -> 0.82 us
    all_gather x1, waiting for transfers between devices: 116 us -> 170 us  [per_device(): gathered = lax.all_gather(arrived, 'seq', axis=0, tiled=False)]
    dynamic_update_slice x40 -> x0, other arithmetic: 43.9 us -> none  [span_scan(): lax.scan(advance, start_state, (x_spans, b_spans, c_spans, g_spans))]
    unnamed x41 -> x22, local copies, waits for them, and re-layouts: 47.9 us -> 6.71 us
    all_to_all x7 -> x1, starting transfers between devices: 35.4 us -> 7.2 us  [per_device(): route = lax.all_to_all(route, SEQ_EXP, 0, 0, tiled=True)]
  transfers between devices with their start and end apart: 11 -> 4, of which waited for: 6 -> 3; matrix products, arithmetic and copies ran while one was open for 48% -> 1% of each run, Pallas kernels for 0% -> 10%
where the time goes in v1:
time: 406 us; the launch traced here: 405 us
  waiting for transfers between devices  179 us (44%)
  Pallas kernels  144 us (35%)
  blocking collectives  31.6 us (8%)
  local copies, waits for them, and re-layouts  16.2 us (4%)
  between operations  15.7 us (4%)
  starting transfers between devices  13.4 us (3%)
    all_gather x1, waiting for transfers between devices, per_device(): gathered = lax.all_gather(arrived, 'seq', axis=0, tiled=False)  170 us
    pallas_call x1, Pallas kernels, ssm_part(): pl.pallas_call(ssm_kernel, out_shape=(jax.ShapeDtypeStruct((4, 4, 4, *in_...  93 us
    pallas_call x1, Pallas kernels, expert_part(): pl.pallas_call(expert_kernel, grid=(slots // step,), out_shape=(jax.Shape...  39.1 us
    all_to_all x1, blocking collectives, per_device(): lax.all_to_all(outgoing, EXP, 0, 0, tiled=True)  31.6 us
    pallas_call x1, Pallas kernels, project(): pl.pallas_call(project_kernel, grid=(8,), out_shape=(half, half), in_spec...  12.1 us
  transfers between devices with their start and end apart: 4, of which 3 were waited for; matrix products, arithmetic and copies ran while one was open for 1% of the time, Pallas kernels for 10%

profile of v1, /device:TPU:1, one launch (start us, length us, event | category | flops | bytes accessed | tf_op | source)
XLA Modules:
  0.0 405.4 jit_solution(7600955485342504416)
XLA Ops:
  8.0 0.0 copy-start
  8.0 0.0 all-gather.2.cloned.1.call-start
  8.1 0.7 exponential_bitcast_fusion.2
  8.8 0.8 broadcast_multiply_fusion.1
  9.7 0.2 fusion.2
  9.9 0.2 slice_reduce_fusion
  10.1 0.1 reshape_squeeze.4
  10.2 0.2 reduce_window_sum.28
  10.3 0.2 exponential_reduce_fusion
  10.5 0.1 copy.55.rate_ref
  10.6 0.7 broadcast_in_dim.30
  11.4 0.1 reshape_reshape.11.skip_ref
  11.4 0.1 broadcast_in_dim.14
  11.5 0.1 reshape.143
  11.6 0.1 copy.53
  11.7 0.1 copy.52
  11.8 0.1 broadcast_in_dim.12
  11.8 0.1 reshape_reshape.9.whole_ref
  11.9 0.1 broadcast_in_dim.13
  12.0 0.1 reshape_reshape.10.before_ref
  12.1 0.4 copy.54.lcol_ref
  12.5 0.0 copy-start.1
  12.5 1.2 copy-done.1
  13.7 1.0 copy-done.3
  14.8 1.0 copy-done.4
  15.8 0.9 copy-done.5
  16.8 93.0 %ssm.1 = (bf16[4,4,4,512,256]{4,3,2,1,0:T(8,128)(2,1)}, bf16[8,256,256]{2,1,0:T(8,128)(2,1)S(1)}, f32[2048,256]{1,0:T(8,128)}, f32[4,2048]{1,0:T(4,128)S(1)}) custom-call(bf16[512,256]{1,0:T(8,128)(2,1)S(1)} %copy-done.5, bf16[2048,256]{1,0:T(8,128)(2,1)S(1)} %copy-done, bf16[2048,256]{1,0:T(8,128)(2,1)S(1)} %copy-done.1, bf16[2048,128]{1,0:T(8,128)(2,1)S(1)} %copy-done.3, ...), custom_call_target="tpu_custom_call" | custom-call | tf_op jit(solution)/shard_map/ssm/pallas_call | solution.py:361
  109.7 0.0 copy-start.2
  109.7 1.0 copy-done.2
  110.7 12.1 %project.1 = (bf16[128,4096]{1,0:T(8,128)(2,1)}, bf16[128,4096]{1,0:T(8,128)(2,1)}) custom-call(s32[1]{0:T(128)} %bitcast.1.core_ref, bf16[8,256,256]{2,1,0:T(8,128)(2,1)} %copy-done.2, bf16[4,2,2,4,512,256]{5,4,3,2,1,0:T(8,128)(2,1)} %bitcast.34), custom_call_target="tpu_custom_call" | custom-call | tf_op jit(solution)/shard_map/project/pallas_call | solution.py:411
  122.8 6.1 %collective-permute-start = (bf16[128,4096]{1,0:T(8,128)(2,1)}, bf16[128,4096]{1,0:T(8,128)(2,1)S(1)}, u32[]{:S(2)}, u32[]{:S(2)}) collective-permute-start(bf16[128,4096]{1,0:T(8,128)(2,1)} %get-tuple-element.16), channel_id=1, source_target_pairs={{0,1},{1,0},{2,3},{3,2},{4,5},{5,4},{6,7},{7,6},{8,9},{9,8},{10,11... | collective-permute-start | bytes 3145736 | tf_op jit(solution)/shard_map/ppermute | solution.py:482
  128.9 0.1 copy.47
  129.1 0.1 eq.45
  129.2 0.1 eq.41
  129.4 0.6 reduce-window.6
  129.9 0.2 slice_reduce_fusion.1
  130.2 0.1 fusion.4
  130.3 0.1 sub.22
  130.4 0.1 copy.51
  130.5 0.1 fusion.1
  130.6 0.1 select_reduce_fusion
  130.8 0.6 collective-permute-done
  131.4 2.0 fusion
  133.4 31.6 %all_to_all.14 = bf16[16,16,4096]{2,1,0:T(8,128)(2,1)} all-to-all(bf16[16,16,4096]{2,1,0:T(8,128)(2,1)S(1)} %bitcast.36), channel_id=1, replica_groups=mesh['seq'=8,'exp_0'=2,'exp_1'=4,'exp_2'=2] {'exp_0','exp_1','exp_2'}, dimensions={0} | all-to-all | bytes 4194304 | tf_op jit(solution)/shard_map/all_to_all | solution.py:493
  165.1 0.0 all-gather.2.cloned.1.call-update
  165.1 0.0 reduce-scatter.2.cloned.1.call-start
  165.1 0.5 reduce-scatter.2.cloned.1.call-update
  165.7 0.1 copy.57
  165.8 0.1 mul.55
  165.9 169.7 %all-gather.2.cloned.1.call-done.a_ref = bf16[8,256,4096]{2,1,0:T(8,128)(2,1)} async-done(((bf16[1,256,4096]{2,1,0:T(8,128)(2,1)}), bf16[8,256,4096]{2,1,0:T(8,128)(2,1)}) %all-gather.2.cloned.1.call-update) | async-done | bytes 16777232 | tf_op jit(solution)/shard_map/all_gather | solution.py:494
  335.6 39.1 %experts.1 = (bf16[2048,2,896]{2,1,0:T(2,128)(2,1)}, f32[8,2048]{1,0:T(8,128)}) custom-call(bf16[8,256,4096]{2,1,0:T(8,128)(2,1)} %all-gather.2.cloned.1.call-done.a_ref, bf16[1,896,4096]{2,1,0:T(8,128)(2,1)} %w_ref.3, bf16[2048,2,896]{2,1,0:T(2,128)(2,1)} %bitcast.37), custom_call_target="tpu_custom_call" | custom-call | tf_op jit(solution)/shard_map/experts/pallas_call | solution.py:446
  374.7 0.9 slice_reduce_fusion.2
  375.6 0.7 all_to_all.10
  376.3 7.2 %all-to-all-start.1 = ((f32[128,1,16]{2,1,0:T(1,128)}), f32[128,1,16]{2,1,0:T(1,128)S(1)}, u32[]{:S(2)}, u32[]{:S(2)}) async-start(f32[128,1,16]{2,1,0:T(1,128)} %bitcast.11), calls=%async_computation.1 | async-start | bytes 131072 | tf_op jit(solution)/shard_map/all_to_all | solution.py:497
  383.5 0.0 reduce-scatter.2.cloned.1.call-done
  383.6 1.5 fusion.10
  385.1 8.0 %all-to-all-done.1 = f32[128,1,16]{2,1,0:T(1,128)S(1)} async-done(((f32[128,1,16]{2,1,0:T(1,128)}), f32[128,1,16]{2,1,0:T(1,128)S(1)}, u32[]{:S(2)}, u32[]{:S(2)}) %all-to-all-start.1) | async-done | bytes 8224 | tf_op jit(solution)/shard_map/all_to_all | solution.py:497
  393.1 0.5 broadcast.97
  393.6 0.8 reduce.13
  394.4 0.1 reshape.146
  394.6 1.9 gather_fusion
  396.5 0.1 reshape.147
  396.7 0.6 copy.58
  397.3 0.6 copy.62
  (24 shorter events, 0.2 us)
Async XLA Ops:
  8.0 4.5 %copy-start = (bf16[2048,256]{1,0:T(8,128)(2,1)S(1)}, bf16[2048,256]{1,0:T(8,128)(2,1)}, u32[]{:S(2)}) copy-start(bf16[2048,256]{1,0:T(8,128)(2,1)} %x_ref.1) | copy-start | bytes 3145732
  8.0 327.6 %all-gather.2.cloned.1.call-start = ((), (), s32[]{:S(2)}) async-start(), calls=%async_computation.3 | async-start | bytes 18874368 | tf_op jit(solution)/shard_map/all_gather | solution.py:494
  12.5 1.2 copy-start.1
  13.7 1.0 copy-start.3
  14.8 1.0 copy-start.4
  15.8 0.9 copy-start.5
  109.7 1.0 copy-start.2
  110.7 18.2 %copy-start.8 = (s32[128,2]{0,1:T(2,128)S(1)}, s32[128,2]{0,1:T(2,128)}, u32[]{:S(2)}) copy-start(s32[128,2]{0,1:T(2,128)} %param.14) | copy-start | bytes 3076
  110.7 19.9 %copy-start.7 = (f32[128,2]{0,1:T(2,128)S(1)}, f32[128,2]{0,1:T(2,128)}, u32[]{:S(2)}) copy-start(f32[128,2]{0,1:T(2,128)} %param.13) | copy-start | bytes 3076
  110.7 20.7 %copy-start.6 = (bf16[128,4096]{1,0:T(8,128)(2,1)S(1)}, bf16[128,4096]{1,0:T(8,128)(2,1)}, u32[]{:S(2)}) copy-start(bf16[128,4096]{1,0:T(8,128)(2,1)} %param.17) | copy-start | bytes 3145732
  122.8 8.6 %collective-permute-start = (bf16[128,4096]{1,0:T(8,128)(2,1)}, bf16[128,4096]{1,0:T(8,128)(2,1)S(1)}, u32[]{:S(2)}, u32[]{:S(2)}) collective-permute-start(bf16[128,4096]{1,0:T(8,128)(2,1)} %get-tuple-element.16), channel_id=1, source_target_pairs={{0,1},{1,0},{2,3},{3,2},{4,5},{5,4},{6,7},{7,6},{8,9},{9,8},{10,11... | collective-permute-start | bytes 3145736 | tf_op jit(solution)/shard_map/ppermute | solution.py:482
  165.1 218.5 %reduce-scatter.2.cloned.1.call-start = ((), (), s32[]{:S(2)}) async-start(), calls=%async_computation.4 | async-start | bytes 2228224 | tf_op jit(solution)/shard_map/reduce_scatter | solution.py:479
  376.3 16.8 %all-to-all-start.1 = ((f32[128,1,16]{2,1,0:T(1,128)}), f32[128,1,16]{2,1,0:T(1,128)S(1)}, u32[]{:S(2)}, u32[]{:S(2)}) async-start(f32[128,1,16]{2,1,0:T(1,128)} %bitcast.11), calls=%async_computation.1 | async-start | bytes 131072 | tf_op jit(solution)/shard_map/all_to_all | solution.py:497
Sparse Core Ops, SparseCore 0:
  165.2 170.3 all-gather.1
Sparse Core Ops, SparseCore 1:
  169.4 198.1 reduce-scatter.1

commit v2 on v1

--- a/solution.py
+++ b/solution.py
@@ -58,6 +58,7 @@
 
 
 ORDERS = ("xyz", "yzx", "zxy", "xzy", "yxz", "zyx")
+SHARES = (5, 6, 5, 5, 5, 6)
 UNIT = 16
 
 
@@ -80,10 +81,7 @@
     def __init__(self, torus, own_ref, out_ref, send_sem, recv_sem):
         self.torus, self.own, self.out = torus, own_ref, out_ref
         self.send_sem, self.recv_sem = send_sem, recv_sem
-        units = own_ref.shape[0] // UNIT
-        count = len(ORDERS)
-        ends = [units * k // count * UNIT for k in range(count + 1)]
-        self.rows = [(ends[k], ends[k + 1] - ends[k]) for k in range(count)]
+        self.rows = [(sum(SHARES[:k]) * UNIT, SHARES[k] * UNIT) for k in range(len(ORDERS))]
 
     def block(self, stream, phase, step, start, size):
         order = ORDERS[stream]
@@ -148,10 +146,10 @@
 
 
 def ssm_kernel(
-    w_ref, x_ref, g_ref, b_ref, c_ref, lcol_ref, lrow_ref, whole_ref, before_ref, tail_ref, skip_ref, rate_ref,
+    w_hbm, x_hbm, g_hbm, b_hbm, c_hbm, lcol_ref, lrow_ref, whole_ref, before_ref, tail_ref, skip_ref, rate_ref,
     all_ref, dx_ref, dbc_ref, dq_ref,
-    s_all, g_all, s_acc, g_acc, ends, got, dx_all,
-    own_sem, w_send, w_recv, s_send, s_recv, x_send, x_recv,
+    w_ref, x_ref, g_ref, b_ref, c_ref, s_all, g_all, s_acc, g_acc, ends, got, dx_all,
+    load_sem, own_sem, w_send, w_recv, s_send, s_recv, x_send, x_recv,
 ):
     chunks = s_all.shape[0]
     parts = got.shape[0]
@@ -167,6 +165,10 @@
     def chip_at(index):
         return {"exp_0": lax.div(index, 4), "exp_1": lax.rem(index, 4)}
 
+    pairs_in = ((w_hbm, w_ref), (x_hbm, x_ref), (g_hbm, g_ref), (b_hbm, b_ref), (c_hbm, c_ref))
+    loads = [pltpu.make_async_copy(a, b, load_sem.at[k]) for k, (a, b) in enumerate(pairs_in)]
+    for load in loads:
+        load.start()
     across_y = {"seq": lax.rem(me + 4, 8), "exp_0": 1 - lax.axis_index("exp_0")}
     barrier_with(
         [{"seq": in_part(o)} for o in range(1, parts)]
@@ -175,6 +177,7 @@
     )
     gather = Gather(torus, w_ref, all_ref, w_send, w_recv)
     streams = range(len(ORDERS))
+    loads[0].wait()
     gather.advance(0, streams)
     here = torus.at
     own = pltpu.make_async_copy(w_ref, all_ref.at[here["x"], here["y"], here["z"]], own_sem.at[0])
@@ -197,6 +200,8 @@
         g_acc[...] = g_acc[...] + before_ref[chunk] * back
         return carry
 
+    for load in loads[1:]:
+        load.wait()
     lax.fori_loop(0, chunks, states, 0)
     ends[0, :128, :] = s_acc[...].astype(BF16)
     ends[1, :128, :] = g_acc[...].astype(BF16)
@@ -366,9 +371,14 @@
             jax.ShapeDtypeStruct((length, 256), F32),
             jax.ShapeDtypeStruct((heads, length), F32),
         ),
-        in_specs=[vmem] * 12,
+        in_specs=[pl.BlockSpec(memory_space=pltpu.HBM)] * 5 + [vmem] * 7,
         out_specs=(hbm, hbm, vmem, vmem),
         scratch_shapes=[
+            pltpu.VMEM(in_weight.shape, BF16),
+            pltpu.VMEM((length, width), BF16),
+            pltpu.VMEM((length, width), BF16),
+            pltpu.VMEM((length, 128), BF16),
+            pltpu.VMEM((length, 128), BF16),
             pltpu.VMEM((chunks, 128, width), F32),
             pltpu.VMEM((chunks, 128, width), F32),
             pltpu.VMEM((128, width), F32),
@@ -376,6 +386,7 @@
             pltpu.VMEM((2, 144, width), BF16),
             pltpu.VMEM((parts, 144, width), BF16),
             pltpu.VMEM((chunks, SPAN, width), BF16),
+            dma((5,)),
             dma((1,)),
             dma((streams, 6, 2)),
             dma((streams, 6, 2)),
@@ -423,47 +434,309 @@
         name="project",
     )(lax.axis_index(CORE).reshape(1).astype(jnp.int32), x_all, w_all)
 
-
-def expert_kernel(a_ref, w_ref, saved_ref, pre_ref, route_ref):
-    rows = a_ref.shape[0] * a_ref.shape[1]
-    upstream = nt(a_ref[...].reshape(rows, a_ref.shape[2]), w_ref[0])
-    gate_pre = saved_ref[:, 0, :].astype(F32)
-    up_pre = saved_ref[:, 1, :].astype(F32)
-    sig = jax.nn.sigmoid(gate_pre)
-    act = gate_pre * sig
-    up_grad = upstream * act
-    gate_grad = upstream * up_pre * sig * (1.0 + gate_pre * (1.0 - sig))
-    pre_ref[:, 0, :] = gate_grad.astype(BF16)
-    pre_ref[:, 1, :] = up_grad.astype(BF16)
-    route_ref[...] = nt(jnp.ones((8, up_pre.shape[1]), BF16), (up_grad * up_pre).astype(BF16))
-
-
-def expert_part(gathered, w_down, saved_pre):
-    parts, own, d = gathered.shape
+def exactly(values, ones):
+    high = values.astype(BF16)
+    low = (values - high.astype(F32)).astype(BF16)
+    ones = ones.astype(F32).astype(BF16)
+    return nn(high, ones) + nn(low, ones)
+
+
+def offset_of(turn):
+    j = lax.rem(turn, 4)
+    return lax.div(turn, 4), j + lax.div(j, 2) * (1 - 2 * lax.rem(j, 2))
+
+
+FIRST_COLUMNS = 1792
+
+
+def expert_kernel(
+    keep_ref, other_ref, residual_ref, select_ref, gate_ref, w_hbm, saved_hbm,
+    pre_hbm, route_ref,
+    rows_out, held, w_ref, saved_buf, pre_buf, shares, part_out, part_in, sum_out, sum_in,
+    w_sem, saved_sem, pre_sem, a_send, a_recv, g_send, g_recv, p_send, p_recv, q_send, q_recv,
+):
+    turns, _, _, block, d = held.shape
+    slots = block // 2
+    hidden = w_ref.shape[0]
+    seq = lax.axis_index("seq")
+    x, y = lax.rem(seq, 4), lax.div(seq, 4)
+    chip_y, chip_z, core = (lax.axis_index(name) for name in EXP)
+    right = {"seq": y * 4 + lax.rem(x + 1, 4)}
+    left = {"seq": y * 4 + lax.rem(x + 3, 4)}
+    facing = {"seq": lax.rem(seq + 4, 8)}
+    x_left, x_right, x_far = lax.rem(x + 3, 4), lax.rem(x + 1, 4), lax.rem(x + 2, 4)
+    mates = [{"exp_2": 1 - core}]
+    for turn in range(1, turns):
+        by, bz = turn // 4, (0, 1, 3, 2)[turn % 4]
+        for k in range(2):
+            mates.append(
+                {
+                    "seq": lax.rem(seq + 4 * by, 8),
+                    "exp_0": lax.rem(chip_y + by, 2),
+                    "exp_1": lax.rem(chip_z + (4 - bz), 4),
+                    "exp_2": k,
+                }
+            )
+    mates += [{"seq": lax.rem(seq + k, 8)} for k in range(1, 8)]
+    mates += [{"exp_0": 1 - chip_y, "exp_1": z, "exp_2": k} for z in range(4) for k in range(2)]
+    barrier_with(mates)
+    load_w = pltpu.make_async_copy(w_hbm.at[0], w_ref, w_sem.at[0])
+    load_w.start()
+
+    def chip_of(turn):
+        by, bz = offset_of(turn)
+        return lax.rem(chip_y + by, 2) * 4 + lax.rem(chip_z + bz, 4)
+
+    def load_saved(turn):
+        slot = lax.rem(turn, 2)
+        return pltpu.make_async_copy(saved_hbm.at[:, chip_of(turn)], saved_buf.at[slot], saved_sem.at[slot])
+
+    def store_pre(turn):
+        slot = lax.rem(turn, 2)
+        return pltpu.make_async_copy(pre_buf.at[slot], pre_hbm.at[:, chip_of(turn)], pre_sem.at[slot])
+
+    load_saved(0).start()
+    moe = (residual_ref[...].astype(F32) + keep_ref[...].astype(F32) + other_ref[...].astype(F32)).astype(BF16)
+    rows = (nn(select_ref[...], moe) * gate_ref[...]).astype(BF16)
+    rows_out[...] = rows.reshape(rows_out.shape)
+    half_of = lambda c: pl.ds(pl.multiple_of(c * slots, slots), slots)
+
+    def first_of(turn):
+        return lax.rem(y + lax.div(turn, 4), 2)
+
+    def to_expert(turn, k):
+        by, bz = turn // 4, (0, 1, 3, 2)[turn % 4]
+        ty, tz = lax.rem(chip_y + by, 2), lax.rem(chip_z + (4 - bz), 4)
+        return pltpu.make_async_remote_copy(
+            src_ref=rows_out.at[(ty * 4 + tz) * 2 + k],
+            dst_ref=held.at[turn, y, x, half_of(core)],
+            send_sem=a_send.at[turn, k],
+            recv_sem=a_recv.at[turn, core],
+            device_id={"seq": lax.rem(seq + 4 * by, 8), "exp_0": ty, "exp_1": tz, "exp_2": k},
+            device_id_type=MESH,
+        )
+
+    def from_source(turn, c):
+        there = held.at[turn, first_of(turn), x, half_of(c)]
+        return pltpu.make_async_remote_copy(
+            src_ref=there, dst_ref=there, send_sem=a_send.at[turn, 0], recv_sem=a_recv.at[turn, c],
+            device_id={"exp_2": 1 - core}, device_id_type=MESH,
+        )
+
+    to_expert(0, 1 - core).start()
+    for turn in range(1, turns):
+        for k in range(2):
+            to_expert(turn, k).start()
+    held[0, y, x, half_of(core), :] = rows_out[(chip_y * 4 + chip_z) * 2 + core]
+
+    first = pl.ds(0, FIRST_COLUMNS)
+    rest = pl.ds(FIRST_COLUMNS, d - FIRST_COLUMNS)
+    low, high, both = pl.ds(0, slots), pl.ds(slots, slots), slice(None)
+
+    def moves(i, step):
+        start = first_of(i)
+        if step == 0:
+            return (
+                (0, held.at[i, start, x, both, first], held.at[i, start, x_left, both, first], right),
+                (1, held.at[i, start, x, both, first], held.at[i, start, x_right, both, first], left),
+                (2, held.at[i, start, x, both, rest], held.at[i, 1 - start, x, both, rest], facing),
+            )
+        if step == 1:
+            return (
+                (3, held.at[i, start, x_left, low, first], held.at[i, start, x_far, low, first], right),
+                (4, held.at[i, start, x_right, high, first], held.at[i, start, x_far, high, first], left),
+                (5, held.at[i, both, x, both, rest], held.at[i, both, x_left, both, rest], right),
+                (6, held.at[i, both, x, both, rest], held.at[i, both, x_right, both, rest], left),
+            )
+        return (
+            (7, held.at[i, start, both, both, first], held.at[i, 1 - start, both, both, first], facing),
+            (8, held.at[i, both, x_left, low, rest], held.at[i, both, x_far, low, rest], right),
+            (9, held.at[i, both, x_right, high, rest], held.at[i, both, x_far, high, rest], left),
+        )
+
+    def each(i, step, act):
+        for number, sent, arriving, peer in moves(i, step):
+            ref = arriving if act == "wait_recv" else sent
+            copy = pltpu.make_async_remote_copy(
+                src_ref=ref, dst_ref=ref, send_sem=g_send.at[i, number], recv_sem=g_recv.at[i, number],
+                device_id=peer, device_id_type=MESH,
+            )
+            getattr(copy, act)()
+
+    def compute(j):
+        slot = lax.rem(j, 2)
+        load_saved(j).wait()
+
+        @pl.when(j < turns - 1)
+        def _():
+            load_saved(j + 1).start()
+
+        @pl.when(j >= 2)
+        def _():
+            store_pre(j - 2).wait()
+
+        count = 8 * block
+        upstream = nt(held[j].reshape(count, d), w_ref[...])
+        gate_pre = saved_buf[slot, :, :, 0, :].astype(F32).reshape(count, hidden)
+        up_pre = saved_buf[slot, :, :, 1, :].astype(F32).reshape(count, hidden)
+        sig = jax.nn.sigmoid(gate_pre)
+        act = gate_pre * sig
+        up_grad = upstream * act
+        gate_grad = upstream * up_pre * sig * (1.0 + gate_pre * (1.0 - sig))
+        pre_buf[slot, :, :, 0, :] = gate_grad.astype(BF16).reshape(8, block, hidden)
+        pre_buf[slot, :, :, 1, :] = up_grad.astype(BF16).reshape(8, block, hidden)
+        store_pre(j).start()
+        sums = nt(jnp.ones((8, hidden), BF16), (up_grad * up_pre).astype(BF16))
+        at = lambda dim, *shape: lax.broadcasted_iota(jnp.int32, shape, dim)
+        sums = jnp.where(lax.div(at(1, 8, count), block) == at(0, 8, count), sums, 0.0)
+        shares[...] += exactly(
+            sums, lax.rem(at(0, count, turns * block), block) + chip_of(j) * block == at(1, count, turns * block)
+        )
+
+    def pass_on(t, carry):
+        @pl.when(t == 0)
+        def _():
+            from_source(0, 1 - core).wait_recv()
+            each(0, 0, "start")
+
+        @pl.when(jnp.logical_and(t >= 1, t < turns))
+        def _():
+            for c in range(2):
+                from_source(t, c).wait_recv()
+            each(t, 0, "start")
+
+        @pl.when(jnp.logical_and(t >= 1, t < turns + 1))
+        def _():
+            each(t - 1, 0, "wait_recv")
+            each(t - 1, 1, "start")
+
+        @pl.when(jnp.logical_and(t >= 2, t < turns + 2))
+        def _():
+            each(t - 2, 1, "wait_recv")
+            each(t - 2, 2, "start")
+
+        @pl.when(t == 2)
+        def _():
+            load_w.wait()
+
+        @pl.when(t >= 3)
+        def _():
+            each(t - 3, 2, "wait_recv")
+            compute(t - 3)
+
+        return carry
+
+    shares[...] = jnp.zeros_like(shares)
+    lax.fori_loop(0, turns + 3, pass_on, 0)
+    all_exp = 16
+    own = (chip_y * 4 + chip_z) * 2 + core
+
+    def exp_device(index):
+        return {"exp_0": lax.div(index, 8), "exp_1": lax.rem(lax.div(index, 2), 4), "exp_2": lax.rem(index, 2)}
+
+    def part(k, back=False):
+        to, source = lax.rem(seq + k, 8), lax.rem(seq + (8 - k), 8)
+        return pltpu.make_async_remote_copy(
+            src_ref=part_in.at[source] if back else part_out.at[to],
+            dst_ref=part_in.at[source] if back else part_in.at[seq],
+            send_sem=p_send.at[k - 1], recv_sem=p_recv.at[k - 1], device_id={"seq": to}, device_id_type=MESH,
+        )
+
+    def total(k, back=False):
+        to, source = lax.rem(own + k, all_exp), lax.rem(own + (all_exp - k), all_exp)
+        return pltpu.make_async_remote_copy(
+            src_ref=sum_in.at[source] if back else sum_out.at[to],
+            dst_ref=sum_in.at[source] if back else sum_in.at[own],
+            send_sem=q_send.at[k - 1], recv_sem=q_recv.at[k - 1], device_id=exp_device(to), device_id_type=MESH,
+        )
+
+    for k in range(8):
+        part_out[k] = shares[k : k + 1, :]
+    for k in range(1, 8):
+        part(k).start()
+    part_in[seq] = part_out[seq]
+    for k in range(1, 8):
+        part(k, back=True).wait_recv()
+    summed = part_in[0]
+    for k in range(1, 8):
+        summed = summed + part_in[k]
+    at = lambda dim, *shape: lax.broadcasted_iota(jnp.int32, shape, dim)
+    width = summed.shape[1]
+    each_exp = jnp.where(lax.div(at(1, all_exp, width), slots) == at(0, all_exp, width), summed, 0.0)
+    each_exp = exactly(each_exp, lax.rem(at(0, width, 128), slots) == at(1, width, 128))
+    for k in range(all_exp):
+        sum_out[k] = each_exp[k : k + 1, :]
+    for k in range(1, all_exp):
+        total(k).start()
+    sum_in[own] = sum_out[own]
+    for k in range(1, all_exp):
+        total(k, back=True).wait_recv()
+    for k in range(all_exp):
+        route_ref[k : k + 1, :] = sum_in[k]
+    for k in range(1, 8):
+        part(k).wait_send()
+    for k in range(1, all_exp):
+        total(k).wait_send()
+    store_pre(turns - 2).wait()
+    store_pre(turns - 1).wait()
+    to_expert(0, 1 - core).wait_send()
+    for turn in range(1, turns):
+        for k in range(2):
+            to_expert(turn, k).wait_send()
+
+    def sent(i, carry):
+        for step in range(3):
+            each(i, step, "wait_send")
+        return carry
+
+    lax.fori_loop(0, turns, sent, 0)
+
+
+def expert_part(keep, other, residual, select, slot_gates, w_down, saved_pre):
     slots, _, hidden = saved_pre.shape[1:]
-    step = 256
-    per = step // own
-    return pl.pallas_call(
+    d = residual.shape[1]
+    rows = select.shape[0]
+    turns, block = 8, rows // 8
+    vmem = pl.BlockSpec(memory_space=pltpu.VMEM)
+    hbm = pl.BlockSpec(memory_space=pl.ANY)
+    dma = pltpu.SemaphoreType.DMA
+    pre, route = pl.pallas_call(
         expert_kernel,
-        grid=(slots // step,),
         out_shape=(
-            jax.ShapeDtypeStruct((slots, 2, hidden), BF16),
-            jax.ShapeDtypeStruct((8, slots), F32),
+            jax.ShapeDtypeStruct((8, turns, block, 2, hidden), BF16),
+            jax.ShapeDtypeStruct((16, 128), F32),
         ),
-        in_specs=[
-            pl.BlockSpec((per, own, d), lambda i: (i, 0, 0)),
-            pl.BlockSpec((1, hidden, d), lambda i: (0, 0, 0)),
-            pl.BlockSpec((step, 2, hidden), lambda i: (i, 0, 0)),
+        in_specs=[vmem] * 5 + [hbm] * 2,
+        out_specs=(hbm, vmem),
+        scratch_shapes=[
+            pltpu.VMEM((16, rows // 16, d), BF16),
+            pltpu.VMEM((turns, 2, 4, block, d), BF16),
+            pltpu.VMEM((hidden, d), BF16),
+            pltpu.VMEM((2, 8, block, 2, hidden), BF16),
+            pltpu.VMEM((2, 8, block, 2, hidden), BF16),
+            pltpu.VMEM((8, turns * block), F32),
+            pltpu.VMEM((8, 1, turns * block), F32),
+            pltpu.VMEM((8, 1, turns * block), F32),
+            pltpu.VMEM((16, 1, 128), F32),
+            pltpu.VMEM((16, 1, 128), F32),
+            dma((1,)),
+            dma((2,)),
+            dma((2,)),
+            dma((turns, 2)),
+            dma((turns, 2)),
+            dma((turns, 10)),
+            dma((turns, 10)),
+            dma((7,)),
+            dma((7,)),
+            dma((15,)),
+            dma((15,)),
         ],
-        out_specs=(
-            pl.BlockSpec((step, 2, hidden), lambda i: (i, 0, 0)),
-            pl.BlockSpec((8, step), lambda i: (0, i)),
-        ),
         compiler_params=pltpu.CompilerParams(
-            dimension_semantics=("arbitrary",), vmem_limit_bytes=60 * 2**20
+            collective_id=2, has_side_effects=True, vmem_limit_bytes=60 * 2**20
         ),
         name="experts",
-    )(gathered, w_down, saved_pre[0])
+    )(keep, other, residual, select, slot_gates, w_down, saved_pre.reshape(8, turns, block, 2, hidden))
+    return pre.reshape(saved_pre.shape), route[:, : block // 2].reshape(-1)
 
 
 def per_device(
@@ -472,15 +745,13 @@
     w_all, x_all, bc_grads, step_grads = ssm_part(
         in_weight, ssm_in, b_proj, c_proj, step_sizes, a_log, skip_gain, ssm_grad
     )
-    tokens_here, d = residual_grad.shape
+    tokens_here = residual_grad.shape[0]
     experts = lax.axis_size(EXP)
-    parts = lax.axis_size("seq")
     capacity = TOPK * tokens_here // experts
     bc_grads = lax.psum_scatter(bc_grads, EXP, scatter_dimension=0, tiled=True)
     b_grads, c_grads = bc_grads[:, :128], bc_grads[:, 128:]
     keep, send = project(x_all, w_all)
     other = lax.ppermute(send, CORE, [(0, 1), (1, 0)])
-    moe_grad = (residual_grad.astype(F32) + keep.astype(F32) + other.astype(F32)).astype(BF16)
     flat_ids = expert_ids.reshape(-1)
     onehot = (flat_ids[:, None] == jnp.arange(experts, dtype=jnp.int32)[None, :]).astype(jnp.int32)
     position = jnp.sum(onehot * jnp.cumsum(onehot, axis=0), axis=1) - 1
@@ -488,16 +759,10 @@
     selector = target[:, None] == jnp.arange(experts * capacity, dtype=jnp.int32)[None, :]
     by_token = selector.reshape(tokens_here, TOPK, -1)
     slot_gates = jnp.sum(by_token * gates[:, :, None], axis=(0, 1))
-    rows = tn(jnp.any(by_token, axis=1).astype(BF16), moe_grad)
-    outgoing = (rows * slot_gates[:, None]).astype(BF16).reshape(experts, capacity, d)
-    arrived = lax.all_to_all(outgoing, EXP, 0, 0, tiled=True).reshape(experts * capacity, d)
-    gathered = lax.all_gather(arrived, "seq", axis=0, tiled=False)
-    pre_grads, route = expert_part(gathered, w_down, saved_pre)
-    route = route[0].reshape(parts * experts, capacity)
-    route = lax.all_to_all(route, SEQ_EXP, 0, 0, tiled=True)
-    totals = jnp.sum(route.reshape(parts, experts * capacity), axis=0)
+    select = jnp.any(by_token, axis=1).astype(BF16).T
+    pre_grads, totals = expert_part(keep, other, residual_grad, select, slot_gates[:, None], w_down, saved_pre)
     route_grads = totals[target].reshape(tokens_here, TOPK) / gates
-    return (pre_grads[None], route_grads, b_grads, c_grads, step_grads)
+    return (pre_grads, route_grads, b_grads, c_grads, step_grads)
 
 
 def solution(mesh):

time: 406 us -> 296 us (0.73)
  waiting for transfers between devices: 179 us -> 0.02 us
  Pallas kernels: 144 us -> 249 us
  blocking collectives: 31.6 us -> 0 us
  starting transfers between devices: 13.4 us -> 3.98 us
  local copies, waits for them, and re-layouts: 16.2 us -> 25.2 us
    all_gather x1 -> x0, waiting for transfers between devices: 170 us -> none  [per_device(): gathered = lax.all_gather(arrived, 'seq', axis=0, tiled=False)]
    pallas_call x1, Pallas kernels: 39.1 us -> 141 us  [expert_part(): pl.pallas_call(expert_kernel, out_shape=(jax.ShapeDtypeStruct((8, turns,...]
    all_to_all x1 -> x0, blocking collectives: 31.6 us -> none  [per_device(): lax.all_to_all(outgoing, EXP, 0, 0, tiled=True)]
    unnamed x22 -> x23, local copies, waits for them, and re-layouts: 6.71 us -> 16.2 us
    all_to_all x1 -> x0, waiting for transfers between devices: 8.04 us -> none  [per_device(): route = lax.all_to_all(route, SEQ_EXP, 0, 0, tiled=True)]
    all_to_all x1 -> x0, starting transfers between devices: 7.2 us -> none  [per_device(): route = lax.all_to_all(route, SEQ_EXP, 0, 0, tiled=True)]
  transfers between devices with their start and end apart: 4 -> 2, of which waited for: 3 -> 0; matrix products, arithmetic and copies ran while one was open for 1% -> 2% of each run, Pallas kernels for 10% -> 52%
where the time goes in v2:
time: 296 us; the launch traced here: 295 us
  Pallas kernels  249 us (84%)
  local copies, waits for them, and re-layouts  25.2 us (9%)
  between operations  14.2 us (5%)
  starting transfers between devices  3.98 us (1%)
    pallas_call x1, Pallas kernels, expert_part(): pl.pallas_call(expert_kernel, out_shape=(jax.ShapeDtypeStruct((8, turns,...  141 us
    pallas_call x1, Pallas kernels, ssm_part(): pl.pallas_call(ssm_kernel, out_shape=(jax.ShapeDtypeStruct((4, 4, 4, *in_...  95.8 us
    unnamed x23, local copies, waits for them, and re-layouts  16.2 us
    pallas_call x1, Pallas kernels, project(): pl.pallas_call(project_kernel, grid=(8,), out_shape=(half, half), in_spec...  12 us
  transfers between devices with their start and end apart: 2, of which 0 were waited for; matrix products, arithmetic and copies ran while one was open for 2% of the time, Pallas kernels for 52%

profile of v2, /device:TPU:1, one launch (start us, length us, event | category | flops | bytes accessed | tf_op | source)
XLA Modules:
  0.0 295.4 jit_solution(15531464469969560025)
XLA Ops:
  7.2 0.0 reduce-scatter.2.cloned.1.call-start
  7.2 0.7 exponential_bitcast_fusion.2
  7.9 0.8 broadcast_multiply_fusion.1
  8.7 0.2 fusion.1
  8.9 0.2 slice_reduce_fusion.1
  9.1 0.1 reshape_squeeze.3
  9.2 0.2 reduce_window_sum.26
  9.4 0.2 exponential_reduce_fusion
  9.6 0.1 broadcast_in_dim.28
  9.7 0.1 reshape.140
  9.8 0.1 copy.37
  9.9 0.1 broadcast_in_dim.13
  9.9 0.1 reshape_reshape.10.before_ref
  10.0 0.1 copy.36
  10.1 0.1 broadcast_in_dim.12
  10.2 0.1 reshape_reshape.9.whole_ref
  10.3 0.4 copy.38.lcol_ref
  10.7 0.1 copy.39.rate_ref
  10.7 0.7 broadcast_in_dim.29
  11.5 0.1 reshape_reshape.11.skip_ref
  11.6 0.0 copy-start
  11.6 1.2 copy-done
  12.8 0.0 copy-start.1
  12.8 1.2 copy-done.1
  14.0 0.0 copy-start.3
  14.0 1.0 copy-done.3
  15.1 0.0 copy-start.4
  15.1 1.0 copy-done.4
  16.1 0.9 copy-done.5
  17.1 95.8 %ssm.1 = (bf16[4,4,4,512,256]{4,3,2,1,0:T(8,128)(2,1)}, bf16[8,256,256]{2,1,0:T(8,128)(2,1)S(1)}, f32[2048,256]{1,0:T(8,128)}, f32[4,2048]{1,0:T(4,128)S(1)}) custom-call(bf16[512,256]{1,0:T(8,128)(2,1)S(1)} %copy-done.5, bf16[2048,256]{1,0:T(8,128)(2,1)S(1)} %copy-done, bf16[2048,256]{1,0:T(8,128)(2,1)S(1)} %copy-done.1, bf16[2048,128]{1,0:T(8,128)(2,1)S(1)} %copy-done.3, ...), custom_call_target="tpu_custom_call" | custom-call | tf_op jit(solution)/shard_map/ssm/pallas_call | solution.py:366
  112.8 0.0 copy-start.2
  112.9 1.0 copy-done.2
  113.8 0.0 reduce-scatter.2.cloned.1.call-update
  113.8 0.0 copy-start.8
  113.9 0.0 copy-start.7
  113.9 12.0 %project.1 = (bf16[128,4096]{1,0:T(8,128)(2,1)}, bf16[128,4096]{1,0:T(8,128)(2,1)}) custom-call(s32[1]{0:T(128)} %bitcast.core_ref, bf16[8,256,256]{2,1,0:T(8,128)(2,1)} %copy-done.2, bf16[4,2,2,4,512,256]{5,4,3,2,1,0:T(8,128)(2,1)} %bitcast.34), custom_call_target="tpu_custom_call" | custom-call | tf_op jit(solution)/shard_map/project/pallas_call | solution.py:422
  125.9 3.9 %collective-permute-start = (bf16[128,4096]{1,0:T(8,128)(2,1)}, bf16[128,4096]{1,0:T(8,128)(2,1)S(1)}, u32[]{:S(2)}, u32[]{:S(2)}) collective-permute-start(bf16[128,4096]{1,0:T(8,128)(2,1)} %get-tuple-element.16), channel_id=1, source_target_pairs={{0,1},{1,0},{2,3},{3,2},{4,5},{5,4},{6,7},{7,6},{8,9},{9,8},{10,11... | collective-permute-start | bytes 3145736 | tf_op jit(solution)/shard_map/ppermute | solution.py:754
  129.9 0.0 copy-done.8
  129.9 0.1 copy.40
  130.0 0.1 eq.41
  130.1 0.1 eq.37
  130.3 0.6 reduce-window.6
  130.9 0.2 slice_reduce_fusion
  131.1 0.1 fusion.3
  131.2 0.1 sub.24
  131.4 0.1 copy.44
  131.4 0.0 copy-done.7
  131.4 0.1 copy.47
  131.5 0.2 select_reduce_fusion
  131.7 0.8 copy.46.gate_ref
  132.5 0.1 fusion
  132.6 0.1 copy.45
  132.7 0.1 mul.45
  132.9 0.6 convert_bitcast_fusion.select_ref
  133.5 0.0 collective-permute-done.other_ref
  133.6 1.0 copy-done.6
  134.5 141.1 %experts.1 = (bf16[8,8,32,2,896]{4,3,2,1,0:T(2,128)(2,1)}, f32[16,128]{1,0:T(8,128)}) custom-call(bf16[128,4096]{1,0:T(8,128)(2,1)} %get-tuple-element.15.keep_ref, bf16[128,4096]{1,0:T(8,128)(2,1)} %copy-done.6, bf16[128,4096]{1,0:T(8,128)(2,1)} %residual_ref.1, bf16[256,128]{1,0:T(8,128)(2,1)} %convert_bitcast_fusion.select_ref, f32[256,1]{1,0:T(8,128)} %copy.46.gate_ref, ...), custom_call_target="tpu_custom_call" | custom-call | tf_op jit(solution)/shard_map/experts/pallas_call | solution.py:703
  275.6 0.8 reshape.145
  276.4 1.9 gather_fusion
  278.4 0.1 reshape.146
  278.5 0.6 copy.48
  279.2 1.5 fusion.9
  280.7 7.3 %copy.53 = bf16[1,2048,2,896]{3,2,1,0:T(2,128)(2,1)} copy(bf16[1,2048,2,896]{3,2,1,0:T(2,128)(2,1)} %bitcast.36) | data formatting | bytes 14680064
  287.9 0.6 copy.54
  (16 shorter events, 0.2 us)
Async XLA Ops:
  7.2 272.0 %reduce-scatter.2.cloned.1.call-start = ((), (), s32[]{:S(2)}) async-start(), calls=%async_computation.1 | async-start | bytes 2228224 | tf_op jit(solution)/shard_map/reduce_scatter | solution.py:751
  11.6 1.2 copy-start
  12.8 1.2 copy-start.1
  14.0 1.0 copy-start.3
  15.1 1.0 copy-start.4
  16.1 0.9 copy-start.5
  112.8 1.0 copy-start.2
  113.8 16.0 %copy-start.8 = (s32[128,2]{0,1:T(2,128)S(1)}, s32[128,2]{0,1:T(2,128)}, u32[]{:S(2)}) copy-start(s32[128,2]{0,1:T(2,128)} %param.14) | copy-start | bytes 3076
  113.9 17.6 %copy-start.7 = (f32[128,2]{0,1:T(2,128)S(1)}, f32[128,2]{0,1:T(2,128)}, u32[]{:S(2)}) copy-start(f32[128,2]{0,1:T(2,128)} %param.13) | copy-start | bytes 3076
  125.9 7.6 %collective-permute-start = (bf16[128,4096]{1,0:T(8,128)(2,1)}, bf16[128,4096]{1,0:T(8,128)(2,1)S(1)}, u32[]{:S(2)}, u32[]{:S(2)}) collective-permute-start(bf16[128,4096]{1,0:T(8,128)(2,1)} %get-tuple-element.16), channel_id=1, source_target_pairs={{0,1},{1,0},{2,3},{3,2},{4,5},{5,4},{6,7},{7,6},{8,9},{9,8},{10,11... | collective-permute-start | bytes 3145736 | tf_op jit(solution)/shard_map/ppermute | solution.py:754
  133.6 1.0 copy-start.6
Sparse Core Ops, SparseCore 0:
  114.0 81.7 reduce-scatter.1

commit v3 on v2

--- a/solution.py
+++ b/solution.py
@@ -190,6 +190,10 @@
     g_acc[...] = jnp.zeros_like(g_acc)
 
     def states(chunk, carry):
+        @pl.when(chunk == 3)
+        def _():
+            gather.advance(1, streams)
+
         rows = rows_of(chunk)
         from_start, to_end = decays(lcol_ref.at[rows])
         fresh = tn(b_ref[rows, :], (x_ref[rows, :].astype(F32) * to_end).astype(BF16))
@@ -222,11 +226,10 @@
     for offset in range(1, parts):
         to_part(offset).start()
     own.wait()
-    gather.advance(1, streams)
+    gather.advance(2, streams)
     got[me] = jnp.zeros(got.shape[1:], BF16)
     for offset in range(1, parts):
         to_part(offset, back=True).wait_recv()
-    gather.advance(2, streams)
 
     def decay_of(m):
         return got[m, 128:129, :].astype(F32) + got[m, 129:130, :].astype(F32)
@@ -298,8 +301,8 @@
         pairs_half = pairs.astype(BF16)
         z = nn(c, s_half)
         v = nn(b, g_half)
-        dbc_ref[rows, :128] = nn(pairs_half, c) + nt(xe, g_half)
-        dbc_ref[rows, 128:] = tn(pairs_half, b) + nt(ge, s_half)
+        dbc_ref[rows, :128] = (nn(pairs_half, c) + nt(xe, g_half)).astype(BF16)
+        dbc_ref[rows, 128:] = (tn(pairs_half, b) + nt(ge, s_half)).astype(BF16)
         dx_all[chunk] = (dx + to_end * v + skip_ref[...] * g.astype(F32)).astype(BF16)
 
         @pl.when(turn < chunks - 1)
@@ -335,7 +338,7 @@
     gather.drain()
 
 
-STEPS_AFTER = ((3, 1), (4, 3))
+STEPS_AFTER = ((3, 0), (4, 3))
 LAST_STEPS = (5, 6)
 
 
@@ -368,7 +371,7 @@
         out_shape=(
             jax.ShapeDtypeStruct((4, 4, 4, *in_weight.shape), BF16),
             jax.ShapeDtypeStruct((chunks, SPAN, width), BF16),
-            jax.ShapeDtypeStruct((length, 256), F32),
+            jax.ShapeDtypeStruct((length, 256), BF16),
             jax.ShapeDtypeStruct((heads, length), F32),
         ),
         in_specs=[pl.BlockSpec(memory_space=pltpu.HBM)] * 5 + [vmem] * 7,
@@ -396,7 +399,7 @@
             dma((chunks - 1,)),
         ],
         compiler_params=pltpu.CompilerParams(
-            collective_id=1, has_side_effects=True, vmem_limit_bytes=48 * 2**20
+            collective_id=1, has_side_effects=True, vmem_limit_bytes=63 * 2**20
         ),
         name="ssm",
     )(in_weight, ssm_in, ssm_grad, b_proj, c_proj, lcol, lrow, whole, before, tail, skip, rates[:, None])
@@ -450,10 +453,10 @@
 
 
 def expert_kernel(
-    keep_ref, other_ref, residual_ref, select_ref, gate_ref, w_hbm, saved_hbm,
-    pre_hbm, route_ref,
-    rows_out, held, w_ref, saved_buf, pre_buf, shares, part_out, part_in, sum_out, sum_in,
-    w_sem, saved_sem, pre_sem, a_send, a_recv, g_send, g_recv, p_send, p_recv, q_send, q_recv,
+    keep_ref, other_ref, residual_ref, select_ref, gate_ref, bc_ref, w_hbm, saved_hbm,
+    pre_hbm, route_ref, b_ref, c_ref,
+    rows_out, held, w_ref, saved_buf, pre_buf, shares, part_out, part_in, sum_out, sum_in, bc_in, bc_sum, bc_other,
+    w_sem, saved_sem, pre_sem, a_send, a_recv, g_send, g_recv, p_send, p_recv, q_send, q_recv, b_send, b_recv,
 ):
     turns, _, _, block, d = held.shape
     slots = block // 2
@@ -593,7 +596,41 @@
             sums, lax.rem(at(0, count, turns * block), block) + chip_of(j) * block == at(1, count, turns * block)
         )
 
+    column = chip_z * 2 + core
+
+    def bc_copy(k, back=False):
+        to, source = lax.rem(column + k, 8), lax.rem(column + (8 - k), 8)
+        return pltpu.make_async_remote_copy(
+            src_ref=bc_in.at[source] if back else bc_ref.at[:, to],
+            dst_ref=bc_in.at[source] if back else bc_in.at[column],
+            send_sem=b_send.at[k], recv_sem=b_recv.at[k],
+            device_id={"exp_1": lax.div(to, 2), "exp_2": lax.rem(to, 2)}, device_id_type=MESH,
+        )
+
+    def bc_half():
+        return pltpu.make_async_remote_copy(
+            src_ref=bc_sum.at[1 - chip_y], dst_ref=bc_other, send_sem=b_send.at[0], recv_sem=b_recv.at[0],
+            device_id={"exp_0": 1 - chip_y}, device_id_type=MESH,
+        )
+
     def pass_on(t, carry):
+        @pl.when(t == 3)
+        def _():
+            for k in range(1, 8):
+                bc_copy(k).start()
+
+        @pl.when(t == 6)
+        def _():
+            bc_in[column] = bc_ref[:, column]
+            for k in range(1, 8):
+                bc_copy(k, back=True).wait_recv()
+            for half in range(2):
+                summed = bc_in[0, half].astype(F32)
+                for k in range(1, 8):
+                    summed = summed + bc_in[k, half].astype(F32)
+                bc_sum[half] = summed
+            bc_half().start()
+
         @pl.when(t == 0)
         def _():
             from_source(0, 1 - core).wait_recv()
@@ -677,6 +714,13 @@
         part(k).wait_send()
     for k in range(1, all_exp):
         total(k).wait_send()
+    bc_half().wait_recv()
+    summed = bc_sum[chip_y] + bc_other[...]
+    b_ref[...] = summed[:, :128]
+    c_ref[...] = summed[:, 128:]
+    bc_half().wait_send()
+    for k in range(1, 8):
+        bc_copy(k).wait_send()
     store_pre(turns - 2).wait()
     store_pre(turns - 1).wait()
     to_expert(0, 1 - core).wait_send()
@@ -692,7 +736,7 @@
     lax.fori_loop(0, turns, sent, 0)
 
 
-def expert_part(keep, other, residual, select, slot_gates, w_down, saved_pre):
+def expert_part(keep, other, residual, select, slot_gates, bc_grads, w_down, saved_pre):
     slots, _, hidden = saved_pre.shape[1:]
     d = residual.shape[1]
     rows = select.shape[0]
@@ -700,14 +744,18 @@
     vmem = pl.BlockSpec(memory_space=pltpu.VMEM)
     hbm = pl.BlockSpec(memory_space=pl.ANY)
     dma = pltpu.SemaphoreType.DMA
-    pre, route = pl.pallas_call(
+    tokens = residual.shape[0]
+    bc_grads = bc_grads.reshape(2, 8, tokens, 256)
+    pre, route, b_grads, c_grads = pl.pallas_call(
         expert_kernel,
         out_shape=(
             jax.ShapeDtypeStruct((8, turns, block, 2, hidden), BF16),
             jax.ShapeDtypeStruct((16, 128), F32),
+            jax.ShapeDtypeStruct((tokens, 128), F32),
+            jax.ShapeDtypeStruct((tokens, 128), F32),
         ),
-        in_specs=[vmem] * 5 + [hbm] * 2,
-        out_specs=(hbm, vmem),
+        in_specs=[vmem] * 6 + [hbm] * 2,
+        out_specs=(hbm, vmem, vmem, vmem),
         scratch_shapes=[
             pltpu.VMEM((16, rows // 16, d), BF16),
             pltpu.VMEM((turns, 2, 4, block, d), BF16),
@@ -719,6 +767,9 @@
             pltpu.VMEM((8, 1, turns * block), F32),
             pltpu.VMEM((16, 1, 128), F32),
             pltpu.VMEM((16, 1, 128), F32),
+            pltpu.VMEM((8, 2, tokens, 256), BF16),
+            pltpu.VMEM((2, tokens, 256), F32),
+            pltpu.VMEM((tokens, 256), F32),
             dma((1,)),
             dma((2,)),
             dma((2,)),
@@ -730,13 +781,15 @@
             dma((7,)),
             dma((15,)),
             dma((15,)),
+            dma((8,)),
+            dma((8,)),
         ],
         compiler_params=pltpu.CompilerParams(
             collective_id=2, has_side_effects=True, vmem_limit_bytes=60 * 2**20
         ),
         name="experts",
-    )(keep, other, residual, select, slot_gates, w_down, saved_pre.reshape(8, turns, block, 2, hidden))
-    return pre.reshape(saved_pre.shape), route[:, : block // 2].reshape(-1)
+    )(keep, other, residual, select, slot_gates, bc_grads, w_down, saved_pre.reshape(8, turns, block, 2, hidden))
+    return pre.reshape(saved_pre.shape), route[:, : block // 2].reshape(-1), b_grads, c_grads
 
 
 def per_device(
@@ -748,8 +801,6 @@
     tokens_here = residual_grad.shape[0]
     experts = lax.axis_size(EXP)
     capacity = TOPK * tokens_here // experts
-    bc_grads = lax.psum_scatter(bc_grads, EXP, scatter_dimension=0, tiled=True)
-    b_grads, c_grads = bc_grads[:, :128], bc_grads[:, 128:]
     keep, send = project(x_all, w_all)
     other = lax.ppermute(send, CORE, [(0, 1), (1, 0)])
     flat_ids = expert_ids.reshape(-1)
@@ -760,7 +811,9 @@
     by_token = selector.reshape(tokens_here, TOPK, -1)
     slot_gates = jnp.sum(by_token * gates[:, :, None], axis=(0, 1))
     select = jnp.any(by_token, axis=1).astype(BF16).T
-    pre_grads, totals = expert_part(keep, other, residual_grad, select, slot_gates[:, None], w_down, saved_pre)
+    pre_grads, totals, b_grads, c_grads = expert_part(
+        keep, other, residual_grad, select, slot_gates[:, None], bc_grads, w_down, saved_pre
+    )
     route_grads = totals[target].reshape(tokens_here, TOPK) / gates
     return (pre_grads, route_grads, b_grads, c_grads, step_grads)
 

time: 296 us -> 274 us (0.926)
  between operations: 14.2 us -> 0.82 us
  local copies, waits for them, and re-layouts: 25.2 us -> 21.8 us
  Pallas kernels: 249 us -> 246 us
    unnamed x23 -> x21, local copies, waits for them, and re-layouts: 16.2 us -> 11 us
  transfers between devices with their start and end apart: 2 -> 1, of which waited for: 0 -> 0; matrix products, arithmetic and copies ran while one was open for 2% -> 1% of each run, Pallas kernels for 52% -> 0%
where the time goes in v3:
time: 274 us; the launch traced here: 273 us
  Pallas kernels  246 us (90%)
  local copies, waits for them, and re-layouts  21.8 us (8%)
  other arithmetic  3.49 us (1%)
    pallas_call x1, Pallas kernels, expert_part(): pl.pallas_call(expert_kernel, out_shape=(jax.ShapeDtypeStruct((8, turns,...  138 us
    pallas_call x1, Pallas kernels, ssm_part(): pl.pallas_call(ssm_kernel, out_shape=(jax.ShapeDtypeStruct((4, 4, 4, *in_...  95.5 us
    pallas_call x1, Pallas kernels, project(): pl.pallas_call(project_kernel, grid=(8,), out_shape=(half, half), in_spec...  12 us
    unnamed x21, local copies, waits for them, and re-layouts  11 us
  transfers between devices with their start and end apart: 1, of which 0 were waited for; matrix products, arithmetic and copies ran while one was open for 1% of the time, Pallas kernels for 0%

profile of v3, /device:TPU:1, one launch (start us, length us, event | category | flops | bytes accessed | tf_op | source)
XLA Modules:
  0.0 273.5 jit_solution(13816682066430122878)
XLA Ops:
  0.6 0.7 exponential_bitcast_fusion.2
  1.3 0.8 broadcast_multiply_fusion.1
  2.2 0.2 fusion.1
  2.4 0.2 slice_reduce_fusion.1
  2.5 0.1 reshape_squeeze.3
  2.6 0.2 reduce_window_sum.26
  2.8 0.2 exponential_reduce_fusion
  3.0 0.0 copy-start.1
  3.1 0.1 broadcast_in_dim.28
  3.1 0.1 reshape.143
  3.2 0.1 copy.37
  3.3 0.1 broadcast_in_dim.13
  3.4 0.7 reshape_reshape.10.before_ref
  4.1 0.1 copy.36
  4.2 0.1 broadcast_in_dim.12
  4.2 0.7 reshape_reshape.9.whole_ref
  4.9 1.3 copy.38.lcol_ref
  6.3 0.7 copy.39.rate_ref
  6.9 0.7 broadcast_in_dim.29
  7.7 0.6 reshape_reshape.11.skip_ref
  8.3 0.6 fusion.7.tail_ref
  8.9 0.0 copy-done.1
  8.9 95.5 %ssm.1 = (bf16[4,4,4,512,256]{4,3,2,1,0:T(8,128)(2,1)}, bf16[8,256,256]{2,1,0:T(8,128)(2,1)}, bf16[2048,256]{1,0:T(8,128)(2,1)}, f32[4,2048]{1,0:T(4,128)}) custom-call(bf16[512,256]{1,0:T(8,128)(2,1)} %w_hbm.2, bf16[2048,256]{1,0:T(8,128)(2,1)} %x_hbm.1, bf16[2048,256]{1,0:T(8,128)(2,1)} %g_hbm.1, bf16[2048,128]{1,0:T(8,128)(2,1)} %b_hbm.1, ...), custom_call_target="tpu_custom_call" | custom-call | tf_op jit(solution)/shard_map/ssm/pallas_call | solution.py:369
  104.5 0.0 copy-start.6
  104.5 0.0 copy-start.5
  104.5 12.0 %project.1 = (bf16[128,4096]{1,0:T(8,128)(2,1)}, bf16[128,4096]{1,0:T(8,128)(2,1)}) custom-call(s32[1]{0:T(128)} %bitcast.core_ref, bf16[8,256,256]{2,1,0:T(8,128)(2,1)} %get-tuple-element.15.x_ref, bf16[4,2,2,4,512,256]{5,4,3,2,1,0:T(8,128)(2,1)} %bitcast.34), custom_call_target="tpu_custom_call" | custom-call | tf_op jit(solution)/shard_map/project/pallas_call | solution.py:425
  116.5 1.4 collective-permute-start
  117.9 0.0 copy-done.6
  117.9 0.1 copy.40
  118.0 0.1 eq.41
  118.2 0.1 eq.37
  118.3 0.6 reduce-window.6
  118.9 0.2 slice_reduce_fusion
  119.1 0.1 fusion.3
  119.2 0.1 sub.24
  119.4 0.1 copy.44
  119.5 0.0 copy-done.5
  119.5 0.1 copy.47
  119.6 0.2 select_reduce_fusion
  119.8 0.8 copy.46.gate_ref
  120.6 0.1 fusion
  120.7 0.1 copy.45
  120.8 0.1 mul.45
  121.0 0.6 convert_bitcast_fusion.select_ref
  121.6 0.0 collective-permute-done.other_ref
  121.6 0.0 copy-start
  121.6 1.0 copy-done
  122.6 138.1 %experts.1 = (bf16[8,8,32,2,896]{4,3,2,1,0:T(2,128)(2,1)}, f32[16,128]{1,0:T(8,128)}, f32[128,128]{1,0:T(8,128)}, f32[128,128]{1,0:T(8,128)}) custom-call(bf16[128,4096]{1,0:T(8,128)(2,1)} %get-tuple-element.17.keep_ref, bf16[128,4096]{1,0:T(8,128)(2,1)} %copy-done, bf16[128,4096]{1,0:T(8,128)(2,1)} %residual_ref.1, ...), custom_call_target="tpu_custom_call" | custom-call | tf_op jit(solution)/shard_map/experts/pallas_call | solution.py:749
  260.7 0.8 reshape.149
  261.5 1.9 gather_fusion
  263.5 0.1 reshape.150
  263.6 0.6 copy.48
  264.3 0.0 copy-start.3
  264.3 0.0 copy-start.2
  264.3 0.0 copy-start.4
  264.3 7.3 %copy.55 = bf16[1,2048,2,896]{3,2,1,0:T(2,128)(2,1)} copy(bf16[1,2048,2,896]{3,2,1,0:T(2,128)(2,1)} %bitcast.36) | data formatting | bytes 14680064
  271.6 0.0 copy-done.3
  271.6 0.6 copy.56
  272.2 0.0 copy-done.2
  272.2 0.6 copy.57
  272.8 0.0 copy-done.4
  272.8 0.6 copy.58
  (12 shorter events, 0.2 us)
Async XLA Ops:
  3.0 5.9 %copy-start.1 = (f32[4,2048]{1,0:T(4,128)}, f32[4,2048]{1,0:T(4,128)S(1)}, u32[]{:S(2)}) copy-start(f32[4,2048]{1,0:T(4,128)S(1)} %reshape.142.lrow_ref) | copy-start | bytes 98308
  104.5 13.5 %copy-start.6 = (s32[128,2]{0,1:T(2,128)S(1)}, s32[128,2]{0,1:T(2,128)}, u32[]{:S(2)}) copy-start(s32[128,2]{0,1:T(2,128)} %param.14) | copy-start | bytes 3076
  104.5 15.0 %copy-start.5 = (f32[128,2]{0,1:T(2,128)S(1)}, f32[128,2]{0,1:T(2,128)}, u32[]{:S(2)}) copy-start(f32[128,2]{0,1:T(2,128)} %param.13) | copy-start | bytes 3076
  116.5 5.1 %collective-permute-start = (bf16[128,4096]{1,0:T(8,128)(2,1)}, bf16[128,4096]{1,0:T(8,128)(2,1)S(1)}, u32[]{:S(2)}, u32[]{:S(2)}) collective-permute-start(bf16[128,4096]{1,0:T(8,128)(2,1)} %get-tuple-element.18), channel_id=1, source_target_pairs={{0,1},{1,0},{2,3},{3,2},{4,5},{5,4},{6,7},{7,6},{8,9},{9,8},{10,11... | collective-permute-start | bytes 3145736 | tf_op jit(solution)/shard_map/ppermute | solution.py:805
  121.6 1.0 copy-start
  264.3 7.3 %copy-start.3 = (f32[128,128]{1,0:T(8,128)S(1)}, f32[128,128]{1,0:T(8,128)}, u32[]{:S(2)}) copy-start(f32[128,128]{1,0:T(8,128)} %get-tuple-element.50) | copy-start | bytes 196612
  264.3 7.9 %copy-start.2 = (f32[128,128]{1,0:T(8,128)S(1)}, f32[128,128]{1,0:T(8,128)}, u32[]{:S(2)}) copy-start(f32[128,128]{1,0:T(8,128)} %get-tuple-element.51) | copy-start | bytes 196612
  264.3 8.6 %copy-start.4 = (f32[4,2048]{1,0:T(4,128)S(1)}, f32[4,2048]{1,0:T(4,128)}, u32[]{:S(2)}) copy-start(f32[4,2048]{1,0:T(4,128)} %get-tuple-element.52) | copy-start | bytes 98308

commit v4 on v3

--- a/solution.py
+++ b/solution.py
@@ -146,9 +146,9 @@
 
 
 def ssm_kernel(
-    w_hbm, x_hbm, g_hbm, b_hbm, c_hbm, lcol_ref, lrow_ref, whole_ref, before_ref, tail_ref, skip_ref, rate_ref,
+    w_hbm, x_hbm, g_hbm, b_hbm, c_hbm, step_hbm, a_ref, skip_ref,
     all_ref, dx_ref, dbc_ref, dq_ref,
-    w_ref, x_ref, g_ref, b_ref, c_ref, s_all, g_all, s_acc, g_acc, ends, got, dx_all,
+    w_ref, x_ref, g_ref, b_ref, c_ref, step_ref, lcol_ref, lrow_ref, whole_ref, before_ref, s_all, g_all, s_acc, g_acc, ends, got, dx_all,
     load_sem, own_sem, w_send, w_recv, s_send, s_recv, x_send, x_recv,
 ):
     chunks = s_all.shape[0]
@@ -165,7 +165,7 @@
     def chip_at(index):
         return {"exp_0": lax.div(index, 4), "exp_1": lax.rem(index, 4)}
 
-    pairs_in = ((w_hbm, w_ref), (x_hbm, x_ref), (g_hbm, g_ref), (b_hbm, b_ref), (c_hbm, c_ref))
+    pairs_in = ((w_hbm, w_ref), (x_hbm, x_ref), (g_hbm, g_ref), (b_hbm, b_ref), (c_hbm, c_ref), (step_hbm, step_ref))
     loads = [pltpu.make_async_copy(a, b, load_sem.at[k]) for k, (a, b) in enumerate(pairs_in)]
     for load in loads:
         load.start()
@@ -206,11 +206,40 @@
 
     for load in loads[1:]:
         load.wait()
+    row = lax.broadcasted_iota(jnp.int32, (SPAN, SPAN), 0)
+    col = lax.broadcasted_iota(jnp.int32, (SPAN, SPAN), 1)
+    rates = [jnp.exp(jnp.full((1, SPAN), a_ref[h], F32)) for h in range(heads)]
+    rate_rows = jnp.concatenate(rates, axis=0)
+    steps = jnp.concatenate([step_ref[:, k * SPAN : (k + 1) * SPAN] * rate_rows for k in range(chunks)], axis=0)
+    until = (row <= col).astype(F32).astype(BF16)
+    high = steps.astype(BF16)
+    rest = steps - high.astype(F32)
+    middle = rest.astype(BF16)
+    low = (rest - middle.astype(F32)).astype(BF16)
+    running = nn(high, until) + nn(middle, until) + nn(low, until)
+    columns = running.T
+    passed = jnp.zeros((1, heads), F32)
+    for k in range(chunks):
+        lrow_ref[:, k * SPAN : (k + 1) * SPAN] = running[k * heads : (k + 1) * heads, :]
+        mine = columns[:, k * heads : (k + 1) * heads]
+        lcol_ref[k * SPAN : (k + 1) * SPAN, :] = mine
+        last = mine[SPAN - 1 : SPAN, :]
+        whole_ref[k] = over_lanes(jnp.exp(-last))
+        before_ref[k] = over_lanes(jnp.exp(-passed))
+        passed = passed + last
+    part_decay = over_lanes(jnp.exp(-passed))
+    high = part_decay.astype(BF16).astype(F32)
+    line = lax.broadcasted_iota(jnp.int32, (16, width), 0)
+    tail = jnp.where(line == 0, high, jnp.where(line == 1, part_decay - high, 0.0)).astype(BF16)
+    lane_head = lax.broadcasted_iota(jnp.int32, (1, width), 1) // HDIM
+    skip = jnp.zeros((1, width), F32)
+    for h in range(heads):
+        skip = jnp.where(lane_head == h, skip_ref[h], skip)
     lax.fori_loop(0, chunks, states, 0)
     ends[0, :128, :] = s_acc[...].astype(BF16)
     ends[1, :128, :] = g_acc[...].astype(BF16)
-    ends[0, 128:, :] = tail_ref[...]
-    ends[1, 128:, :] = tail_ref[...]
+    ends[0, 128:, :] = tail
+    ends[1, 128:, :] = tail
 
     def to_part(offset, back=False):
         peer = in_part(offset)
@@ -249,8 +278,6 @@
         g_all[k] = state
         state = state * whole_ref[k] + fresh
 
-    row = lax.broadcasted_iota(jnp.int32, (SPAN, SPAN), 0)
-    col = lax.broadcasted_iota(jnp.int32, (SPAN, SPAN), 1)
     head_of = lax.broadcasted_iota(jnp.int32, (8, width), 1) // HDIM
     pick = (head_of == lax.broadcasted_iota(jnp.int32, (8, width), 0)).astype(F32)
     pick_half = pick.astype(BF16)
@@ -303,7 +330,7 @@
         v = nn(b, g_half)
         dbc_ref[rows, :128] = (nn(pairs_half, c) + nt(xe, g_half)).astype(BF16)
         dbc_ref[rows, 128:] = (tn(pairs_half, b) + nt(ge, s_half)).astype(BF16)
-        dx_all[chunk] = (dx + to_end * v + skip_ref[...] * g.astype(F32)).astype(BF16)
+        dx_all[chunk] = (dx + to_end * v + skip * g.astype(F32)).astype(BF16)
 
         @pl.when(turn < chunks - 1)
         def _():
@@ -315,7 +342,7 @@
         ones = jnp.ones((width, SPAN), BF16)
         dq = nn(rc.astype(BF16), from_row) + nn(cc.astype(BF16), before_row) + nn((pick * across).astype(BF16), ones)
         for h in range(heads):
-            dq_ref[h : h + 1, rows] = -(dq[h : h + 1, :] + inside[h]) * rate_ref[h : h + 1, :]
+            dq_ref[h : h + 1, rows] = -(dq[h : h + 1, :] + inside[h]) * rates[h]
         for step, after in STEPS_AFTER:
 
             @pl.when(turn == after)
@@ -347,21 +374,6 @@
     heads = width // HDIM
     chunks = length // SPAN
     parts = lax.axis_size("seq")
-    rates = jnp.exp(a_log)
-    steps = (step_sizes * rates[:, None]).reshape(heads * chunks, SPAN)
-    at = jnp.arange(SPAN)
-    lrow = jnp.dot(steps, (at[:, None] <= at[None, :]).astype(F32), precision=lax.Precision.HIGHEST)
-    totals = lrow[:, -1].reshape(heads, chunks)
-    lrow = lrow.reshape(heads, length)
-    lcol = lrow.T
-    whole = jnp.repeat(jnp.exp(-totals).T, HDIM, axis=1).reshape(chunks, 1, width)
-    sums = jnp.cumsum(totals, axis=1)
-    before = jnp.repeat(jnp.exp(-(sums - totals)).T, HDIM, axis=1).reshape(chunks, 1, width)
-    device_decay = jnp.repeat(jnp.exp(-sums[:, -1]), HDIM)
-    skip = jnp.repeat(skip_gain, HDIM).reshape(1, width)
-    high = device_decay.astype(BF16)
-    low = (device_decay - high.astype(F32)).astype(BF16)
-    tail = jnp.pad(jnp.stack([high, low]), ((0, 14), (0, 0)))
     vmem = pl.BlockSpec(memory_space=pltpu.VMEM)
     hbm = pl.BlockSpec(memory_space=pl.ANY)
     streams = len(ORDERS)
@@ -374,7 +386,7 @@
             jax.ShapeDtypeStruct((length, 256), BF16),
             jax.ShapeDtypeStruct((heads, length), F32),
         ),
-        in_specs=[pl.BlockSpec(memory_space=pltpu.HBM)] * 5 + [vmem] * 7,
+        in_specs=[pl.BlockSpec(memory_space=pltpu.HBM)] * 6 + [pl.BlockSpec(memory_space=pltpu.SMEM)] * 2,
         out_specs=(hbm, hbm, vmem, vmem),
         scratch_shapes=[
             pltpu.VMEM(in_weight.shape, BF16),
@@ -382,6 +394,11 @@
             pltpu.VMEM((length, width), BF16),
             pltpu.VMEM((length, 128), BF16),
             pltpu.VMEM((length, 128), BF16),
+            pltpu.VMEM((heads, length), F32),
+            pltpu.VMEM((length, heads), F32),
+            pltpu.VMEM((heads, length), F32),
+            pltpu.VMEM((chunks, 1, width), F32),
+            pltpu.VMEM((chunks, 1, width), F32),
             pltpu.VMEM((chunks, 128, width), F32),
             pltpu.VMEM((chunks, 128, width), F32),
             pltpu.VMEM((128, width), F32),
@@ -389,7 +406,7 @@
             pltpu.VMEM((2, 144, width), BF16),
             pltpu.VMEM((parts, 144, width), BF16),
             pltpu.VMEM((chunks, SPAN, width), BF16),
-            dma((5,)),
+            dma((6,)),
             dma((1,)),
             dma((streams, 6, 2)),
             dma((streams, 6, 2)),
@@ -402,19 +419,29 @@
             collective_id=1, has_side_effects=True, vmem_limit_bytes=63 * 2**20
         ),
         name="ssm",
-    )(in_weight, ssm_in, ssm_grad, b_proj, c_proj, lcol, lrow, whole, before, tail, skip, rates[:, None])
-
-
-def project_kernel(core_ref, x_ref, w_ref, keep_ref, send_ref, total):
+    )(in_weight, ssm_in, ssm_grad, b_proj, c_proj, step_sizes, a_log, skip_gain)
+
+
+def project_kernel(core_ref, x_ref, w_hbm, keep_ref, send_ref, w_ref, total, sem):
     core = core_ref[0]
     half = keep_ref.shape[0]
-    width = x_ref.shape[2]
-    acc = jnp.zeros(total.shape, F32)
-    for k in range(x_ref.shape[0]):
-        acc = acc + nt(x_ref[k], w_ref[0, k // 4, 0, k % 4])
-    total[...] = acc
-    keep_ref[...] = total[pl.ds(pl.multiple_of(core * half, half), half), :].astype(BF16)
-    send_ref[...] = total[pl.ds(pl.multiple_of((1 - core) * half, half), half), :].astype(BF16)
+    rows = w_ref.shape[3]
+    blocks = w_ref.shape[0]
+
+    def load(i):
+        return pltpu.make_async_copy(w_hbm.at[i % 4, :, i // 4], w_ref.at[i], sem.at[i])
+
+    for i in range(blocks):
+        load(i).start()
+    for i in range(blocks):
+        load(i).wait()
+        acc = jnp.zeros(total.shape, F32)
+        for k in range(x_ref.shape[0]):
+            acc = acc + nt(x_ref[k], w_ref[i, k // 4, k % 4])
+        total[...] = acc
+        columns = slice(i * rows, (i + 1) * rows)
+        keep_ref[:, columns] = total[pl.ds(pl.multiple_of(core * half, half), half), :].astype(BF16)
+        send_ref[:, columns] = total[pl.ds(pl.multiple_of((1 - core) * half, half), half), :].astype(BF16)
 
 
 def project(x_all, w_all):
@@ -422,20 +449,21 @@
     rows = w_all.shape[3]
     w_all = w_all.reshape(4, 2, 2, 4, rows, width)
     half = jax.ShapeDtypeStruct((tokens // 2, 8 * rows), BF16)
+    vmem = pl.BlockSpec(memory_space=pltpu.VMEM)
     return pl.pallas_call(
         project_kernel,
-        grid=(8,),
         out_shape=(half, half),
-        in_specs=[
-            pl.BlockSpec(memory_space=pltpu.SMEM),
-            pl.BlockSpec((blocks, tokens, width), lambda i: (0, 0, 0)),
-            pl.BlockSpec((1, 2, 1, 4, rows, width), lambda i: (i % 4, 0, i // 4, 0, 0, 0)),
+        in_specs=[pl.BlockSpec(memory_space=pltpu.SMEM), vmem, pl.BlockSpec(memory_space=pltpu.HBM)],
+        out_specs=(vmem, vmem),
+        scratch_shapes=[
+            pltpu.VMEM((8, 2, 4, rows, width), BF16),
+            pltpu.VMEM((tokens, rows), F32),
+            pltpu.SemaphoreType.DMA((8,)),
         ],
-        out_specs=(pl.BlockSpec((tokens // 2, rows), lambda i: (0, i)),) * 2,
-        scratch_shapes=[pltpu.VMEM((tokens, rows), F32)],
-        compiler_params=pltpu.CompilerParams(dimension_semantics=("arbitrary",)),
+        compiler_params=pltpu.CompilerParams(vmem_limit_bytes=48 * 2**20),
         name="project",
     )(lax.axis_index(CORE).reshape(1).astype(jnp.int32), x_all, w_all)
+
 
 def exactly(values, ones):
     high = values.astype(BF16)

time: 274 us -> 263 us (0.960)
  Pallas kernels: 246 us -> 241 us
  local copies, waits for them, and re-layouts: 21.8 us -> 17.8 us
    pallas_call x1, Pallas kernels: 12 us -> 7.81 us  [project(): pl.pallas_call(project_kernel, out_shape=(half, half), in_specs=[pl.Block...]
    unnamed x21 -> x23, local copies, waits for them, and re-layouts: 11 us -> 13.2 us
where the time goes in v4:
time: 263 us
  Pallas kernels  241 us (92%)
  local copies, waits for them, and re-layouts  17.8 us (7%)
    pallas_call x1, Pallas kernels, expert_part(): pl.pallas_call(expert_kernel, out_shape=(jax.ShapeDtypeStruct((8, turns,...  138 us
    pallas_call x1, Pallas kernels, ssm_part(): pl.pallas_call(ssm_kernel, out_shape=(jax.ShapeDtypeStruct((4, 4, 4, *in_...  95.2 us
    unnamed x23, local copies, waits for them, and re-layouts  13.2 us
    pallas_call x1, Pallas kernels, project(): pl.pallas_call(project_kernel, out_shape=(half, half), in_specs=[pl.Block...  7.81 us
  transfers between devices with their start and end apart: 1, of which 0 were waited for; matrix products, arithmetic and copies ran while one was open for 1% of the time, Pallas kernels for 0%

profile of v4, /device:TPU:1, one launch (start us, length us, event | category | flops | bytes accessed | tf_op | source)
XLA Modules:
  0.0 262.7 jit_solution(9501485602013156286)
XLA Ops:
  0.6 95.2 %ssm.1 = (bf16[4,4,4,512,256]{4,3,2,1,0:T(8,128)(2,1)}, bf16[8,256,256]{2,1,0:T(8,128)(2,1)}, bf16[2048,256]{1,0:T(8,128)(2,1)}, f32[4,2048]{1,0:T(4,128)}) custom-call(bf16[512,256]{1,0:T(8,128)(2,1)} %w_hbm.2, bf16[2048,256]{1,0:T(8,128)(2,1)} %x_hbm.1, bf16[2048,256]{1,0:T(8,128)(2,1)} %g_hbm.1, bf16[2048,128]{1,0:T(8,128)(2,1)} %b_hbm.1, ...), custom_call_target="tpu_custom_call" | custom-call | tf_op jit(solution)/shard_map/ssm/pallas_call | solution.py:381
  95.8 0.0 copy-start.1
  95.8 1.2 copy-done.1
  97.0 0.0 copy-start.7
  97.0 0.0 copy-start.6
  97.1 7.8 %project.1 = (bf16[128,4096]{1,0:T(8,128)(2,1)S(1)}, bf16[128,4096]{1,0:T(8,128)(2,1)S(1)}) custom-call(s32[1]{0:T(128)} %bitcast.core_ref, bf16[8,256,256]{2,1,0:T(8,128)(2,1)S(1)} %copy-done.1, bf16[4,2,2,4,512,256]{5,4,3,2,1,0:T(8,128)(2,1)} %bitcast.26), custom_call_target="tpu_custom_call" | custom-call | tf_op jit(solution)/shard_map/project/pallas_call | solution.py:453
  104.9 0.0 copy-start
  104.9 1.0 copy-done
  105.8 1.4 collective-permute-start
  107.2 0.0 copy-done.7
  107.2 0.1 copy.28
  107.4 0.1 eq.39
  107.5 0.1 eq.43
  107.6 0.6 reduce-window.6
  108.2 0.2 slice_reduce_fusion
  108.5 0.1 fusion.2
  108.6 0.1 sub.9
  108.7 0.1 copy.32
  108.8 0.1 fusion
  108.9 0.1 copy.33
  109.1 0.0 copy-done.6
  109.1 0.1 copy.35
  109.2 0.1 select_reduce_fusion
  109.3 0.8 copy.34.gate_ref
  110.1 0.1 mul.35
  110.3 0.6 convert_bitcast_fusion.select_ref
  110.9 0.0 collective-permute-done.other_ref
  110.9 0.0 copy-start.2
  110.9 1.0 copy-done.2
  111.9 138.0 %experts.1 = (bf16[8,8,32,2,896]{4,3,2,1,0:T(2,128)(2,1)}, f32[16,128]{1,0:T(8,128)}, f32[128,128]{1,0:T(8,128)}, f32[128,128]{1,0:T(8,128)}) custom-call(bf16[128,4096]{1,0:T(8,128)(2,1)} %copy-done, bf16[128,4096]{1,0:T(8,128)(2,1)} %copy-done.2, bf16[128,4096]{1,0:T(8,128)(2,1)} %residual_ref.1, bf16[256,128]{1,0:T(8,128)(2,1)} %convert_bitcast_fusion.select_ref, ...), custom_call_target="tpu_custom_call" | custom-call | tf_op jit(solution)/shard_map/experts/pallas_call | solution.py:777
  250.0 0.8 reshape.105
  250.7 1.9 gather_fusion
  252.7 0.1 reshape.106
  252.9 0.6 copy.36
  253.5 0.0 copy-start.4
  253.5 0.0 copy-start.3
  253.5 0.0 copy-start.5
  253.5 7.3 %copy.43 = bf16[1,2048,2,896]{3,2,1,0:T(2,128)(2,1)} copy(bf16[1,2048,2,896]{3,2,1,0:T(2,128)(2,1)} %bitcast.28) | data formatting | bytes 14680064
  260.8 0.0 copy-done.4
  260.8 0.6 copy.44
  261.4 0.0 copy-done.3
  261.4 0.6 copy.45
  262.1 0.0 copy-done.5
  262.1 0.6 copy.46
  (8 shorter events, 0.1 us)
Async XLA Ops:
  95.8 1.2 copy-start.1
  97.0 10.2 %copy-start.7 = (s32[128,2]{0,1:T(2,128)S(1)}, s32[128,2]{0,1:T(2,128)}, u32[]{:S(2)}) copy-start(s32[128,2]{0,1:T(2,128)} %param.14) | copy-start | bytes 3076
  97.0 12.0 %copy-start.6 = (f32[128,2]{0,1:T(2,128)S(1)}, f32[128,2]{0,1:T(2,128)}, u32[]{:S(2)}) copy-start(f32[128,2]{0,1:T(2,128)} %param.13) | copy-start | bytes 3076
  104.9 1.0 copy-start
  105.8 5.1 %collective-permute-start = (bf16[128,4096]{1,0:T(8,128)(2,1)S(1)}, bf16[128,4096]{1,0:T(8,128)(2,1)S(1)}, u32[]{:S(2)}, u32[]{:S(2)}) collective-permute-start(bf16[128,4096]{1,0:T(8,128)(2,1)S(1)} %get-tuple-element.18), channel_id=1, source_target_pairs={{0,1},{1,0},{2,3},{3,2},{4,5},{5,4},{6,7},{7,6},{8,9},{9,8},{10,11... | collective-permute-start | bytes 3145736 | tf_op jit(solution)/shard_map/ppermute | solution.py:833
  110.9 1.0 copy-start.2
  253.5 7.3 %copy-start.4 = (f32[128,128]{1,0:T(8,128)S(1)}, f32[128,128]{1,0:T(8,128)}, u32[]{:S(2)}) copy-start(f32[128,128]{1,0:T(8,128)} %get-tuple-element.44) | copy-start | bytes 196612
  253.5 7.9 %copy-start.3 = (f32[128,128]{1,0:T(8,128)S(1)}, f32[128,128]{1,0:T(8,128)}, u32[]{:S(2)}) copy-start(f32[128,128]{1,0:T(8,128)} %get-tuple-element.45) | copy-start | bytes 196612
  253.5 8.6 %copy-start.5 = (f32[4,2048]{1,0:T(4,128)S(1)}, f32[4,2048]{1,0:T(4,128)}, u32[]{:S(2)}) copy-start(f32[4,2048]{1,0:T(4,128)} %get-tuple-element.46) | copy-start | bytes 98308
